TPU v7x, 128 devices: a whole 4x4x4 slice. The times are simulated.
128 devices in a mesh: lat: 8 (over z, core), lon: 16 (over x, y).
Axes of the slice: x: 4, y: 4, z: 4, core: 2. Of those that a mesh axis runs over, the one named last changes fastest.
Arguments:
- observations: bfloat16 [196608, 128], P(('lat', 'lon')), may hold values from -6 to 6
- owner_device: int32 [196608, 1], P(('lat', 'lon')), may hold values from 0 to 127; in each aligned block of 1536 rows (0 to 1535, 1536 to 3071, ...) at most 24 rows name the same one
- local_cell: int32 [196608], P(('lat', 'lon')), may hold values from 0 to 383
- valid_counts: int32 [128], P(('lat', 'lon')), may hold values from 768 to 1536
- weight_in: bfloat16 [128, 256], replicated, may hold values from -0.5 to 0.5
- bias_in: float32 [256], replicated, may hold values from -3 to 3
- weight_out: bfloat16 [256, 256], replicated, may hold values from -0.375 to 0.375
- kernel_taps: float32 [9, 256], replicated, may hold values from -2 to 2
- cotangent: bfloat16 [128, 384, 256], P(('lat', 'lon')), may hold values from -6 to 6
Outputs:
- grid_out: bfloat16 [128, 384, 256], P(('lat', 'lon'))
- grad_weight_in: float32 [128, 256], replicated
- grad_bias_in: float32 [256], replicated
- grad_weight_out: float32 [256, 256], replicated
- grad_kernel: float32 [9, 256], replicated
Inputs may be any that keep to these rules, and one draw needn't show every extreme that they name: `owner_device`: within the rows of one block, at most 24 rows name one owner, and in every draw some block names some owner exactly 24 times.
All inputs are finite; a program needn't handle non-finite values.
Results may differ from a plain program's by a relative error of at most 0.0065.
Values may be sent and summed in bfloat16 or wider, within the bound.
A program may use at most 64 MiB of HBM per device.

v0:
```python
import math

import jax
import jax.numpy as jnp
from jax import lax
from jax.sharding import Mesh
from jax.sharding import PartitionSpec as P

LAT = ("lat_0", "lat_1")
LON = ("lon_0", "lon_1")
LAT_LON = ("lat_0", "lat_1", "lon_0", "lon_1")


OFFSETS = [(shift_lat, shift_lon) for shift_lat in (-1, 0, 1) for shift_lon in (-1, 0, 1)]


def extended(shard, sides, width):
    for axis, dim in sides:
        count, length = (lax.axis_size(axis), shard.shape[dim])
        up = [(i, (i + 1) % count) for i in range(count)]
        down = [(j, i) for i, j in up]
        last = lax.slice_in_dim(shard, length - width, length, axis=dim)
        first = lax.slice_in_dim(shard, 0, width, axis=dim)
        before = lax.ppermute(last, axis, up)
        after = lax.ppermute(first, axis, down)
        shard = jnp.concatenate([before, shard, after], axis=dim)
    return shard


def rows_for(lines, count):
    spare = -lines.shape[0] % count
    if not spare:
        return lines
    return jnp.concatenate([lines, jnp.zeros((spare, *lines.shape[1:]), lines.dtype)])


def copy_for_each(shard, axis):
    count = lax.axis_size(axis)
    return lax.all_to_all(
        jnp.broadcast_to(shard[None], (count, *shard.shape)), axis, 0, 0, tiled=True
    )


def laid_out(blocks, dim):
    blocks = jnp.moveaxis(blocks, 0, dim)
    dims = blocks.shape
    return blocks.reshape(*dims[:dim], dims[dim] * dims[dim + 1], *dims[dim + 2 :])


def whole_of(shard, axes, dim):
    far, near = axes
    first = copy_for_each(shard, far)
    blocks = jnp.swapaxes(copy_for_each(first, near), 0, 1)
    return laid_out(blocks.reshape(-1, *shard.shape), dim)


def in_blocks(shard, dim, count):
    before, after = (shard.shape[:dim], shard.shape[dim + 1 :])
    return jnp.moveaxis(shard.reshape(*before, count, -1, *after), dim, 0)


def sum_at_owner(shard, axis, dim):
    count = lax.axis_size(axis)
    blocks = lax.all_to_all(in_blocks(shard, dim, count), axis, 0, 0, tiled=True)
    return jnp.sum(blocks, axis=0)


def summed_rows(shard, axes, dim):
    far, near = axes
    blocks = in_blocks(shard, dim, lax.axis_size(far))
    nearer = sum_at_owner(blocks, near, dim + 1)
    arrived = lax.all_to_all(nearer, far, split_axis=0, concat_axis=0, tiled=True)
    return arrived.sum(axis=0)


def nested_sum(shard, axes):
    padded = rows_for(shard, lax.axis_size(axes[0]) * lax.axis_size(axes[1]))
    whole = whole_of(summed_rows(padded, axes, 0), axes, 0)
    return lax.slice_in_dim(whole, 0, len(shard)).reshape(shard.shape)


def together(arrays, axis):
    line, at, outs = (jnp.concatenate([a.reshape(-1) for a in arrays]), 0, [])
    running = nested_sum(line, axis)
    for a in arrays:
        outs.append(running[at : at + a.size].reshape(a.shape))
        at += a.size
    return tuple(outs)


def encoder(rows, weight_in, bias_in, weight_out):
    before = jnp.dot(rows, weight_in, preferred_element_type=jnp.float32) + bias_in
    hidden = jax.nn.gelu(before).astype(jnp.bfloat16)
    encoded = jnp.dot(hidden, weight_out, preferred_element_type=jnp.float32).astype(jnp.bfloat16)
    return (before, hidden, encoded)


def local_grads(rows, before, hidden, upstream, weight_out):
    contract = (((0,), (0,)), ((), ()))
    grad_out = lax.dot_general(hidden, upstream, contract, preferred_element_type=jnp.float32)
    back = lax.dot_general(
        upstream, weight_out, (((1,), (1,)), ((), ())), preferred_element_type=jnp.float32
    )
    _, pullback = jax.vjp(jax.nn.gelu, before)
    pre_grad = pullback(back)[0].astype(jnp.bfloat16)
    grad_in = lax.dot_general(rows, pre_grad, contract, preferred_element_type=jnp.float32)
    grad_bias = jnp.sum(pre_grad.astype(jnp.float32), axis=0)
    return (grad_in, grad_bias, grad_out)


def edge_mask(padded, tile_rows):
    lat_count = lax.axis_size(LAT)
    lat_here = lax.axis_index(LAT)
    row_ids = jnp.arange(tile_rows + 2, dtype=jnp.int32)
    outside = (row_ids == 0) & (lat_here == 0) | (row_ids == tile_rows + 1) & (
        lat_here == lat_count - 1
    )
    keep_rows = jnp.logical_not(outside).astype(padded.dtype)
    return padded * keep_rows[:, None, None]


def local(
    observations,
    owner_device,
    local_cell,
    valid_counts,
    weight_in,
    bias_in,
    weight_out,
    kernel_taps,
    cotangent,
):
    lat_count = lax.axis_size(LAT)
    lon_count = lax.axis_size(LON)
    devices_all = lat_count * lon_count
    obs_rows = observations.shape[0]
    channels = weight_out.shape[1]
    capacity = 2 * obs_rows // devices_all
    tile_rows = cotangent.shape[0] * lon_count
    tile_cols = cotangent.shape[1] // lon_count
    cells_tile = tile_rows * tile_cols
    owners = owner_device[:, 0]
    valid_rows = jnp.arange(obs_rows, dtype=jnp.int32) < valid_counts[0]
    matches = (owners[:, None] == jnp.arange(devices_all, dtype=jnp.int32)[None, :]).astype(
        jnp.int32
    )
    earlier = jnp.sum((jnp.cumsum(matches, axis=0) - 1) * matches, axis=1)
    slot_index = owners * capacity + earlier
    sent_cells = jnp.full((devices_all * capacity,), cells_tile, jnp.int32)
    sent_cells = sent_cells.at[slot_index].set(jnp.where(valid_rows, local_cell, cells_tile))
    got_cells = lax.all_to_all(
        sent_cells.reshape(devices_all, capacity), LAT_LON, split_axis=0, concat_axis=0, tiled=True
    ).reshape(-1)
    width = observations.shape[1]
    outgoing = (
        jnp.zeros((devices_all * capacity, width), observations.dtype)
        .at[slot_index]
        .set(observations)
    )
    arrived = lax.all_to_all(
        outgoing.reshape(devices_all, capacity, width),
        LAT_LON,
        split_axis=0,
        concat_axis=0,
        tiled=True,
    )
    arrived_rows = arrived.reshape(devices_all * capacity, width)
    before, hidden, arrived_enc = encoder(arrived_rows, weight_in, bias_in, weight_out)
    deposit = jax.ops.segment_sum(
        arrived_enc.astype(jnp.float32), got_cells, num_segments=cells_tile + 1
    )
    deposit = deposit[:cells_tile].reshape(tile_rows, tile_cols, channels)
    padded = extended(deposit, ((LAT, 0), (LON, 1)), 1)
    padded = edge_mask(padded, tile_rows)
    grid_field = jnp.zeros((tile_rows, tile_cols, channels), jnp.float32)
    for tap_index, (shift_lat, shift_lon) in enumerate(OFFSETS):
        window = padded[
            1 + shift_lat : 1 + shift_lat + tile_rows, 1 + shift_lon : 1 + shift_lon + tile_cols
        ]
        grid_field = grid_field + kernel_taps[tap_index] * window
    grid_out = lax.all_to_all(
        grid_field.astype(jnp.bfloat16), LON, split_axis=0, concat_axis=1, tiled=True
    )
    loss_scale = 1.0 / math.sqrt(obs_rows * devices_all)
    cot_tile = lax.all_to_all(cotangent, LON, split_axis=1, concat_axis=0, tiled=True)
    cot_float = cot_tile.astype(jnp.float32)
    cot_padded = extended(cot_tile, ((LAT, 0), (LON, 1)), 1)
    cot_padded = edge_mask(cot_padded, tile_rows).astype(jnp.float32)
    kernel_rows = []
    adjoint = jnp.zeros((tile_rows, tile_cols, channels), jnp.float32)
    for tap_index, (shift_lat, shift_lon) in enumerate(OFFSETS):
        window = padded[
            1 + shift_lat : 1 + shift_lat + tile_rows, 1 + shift_lon : 1 + shift_lon + tile_cols
        ]
        kernel_rows.append(loss_scale * jnp.sum(cot_float * window, axis=(0, 1)))
        back_window = cot_padded[
            1 - shift_lat : 1 - shift_lat + tile_rows, 1 - shift_lon : 1 - shift_lon + tile_cols
        ]
        adjoint = adjoint + kernel_taps[tap_index] * back_window
    grad_kernel = jnp.stack(kernel_rows)
    adjoint = (loss_scale * adjoint).astype(jnp.bfloat16)
    adjoint_rows = jnp.concatenate(
        [adjoint.reshape(cells_tile, channels), jnp.zeros((1, channels), jnp.bfloat16)], axis=0
    )
    upstream = adjoint_rows[got_cells]
    grads = local_grads(arrived_rows, before, hidden, upstream, weight_out)
    grad_in, grad_bias, grad_out, grad_kernel = together(
        (grads[0], grads[1], grads[2], grad_kernel), (("lat_0", "lat_1", "lon_0"), "lon_1")
    )
    return (grid_out, grad_in, grad_bias, grad_out, grad_kernel)


def solution(mesh):
    finer = Mesh(mesh.devices.reshape(4, 2, 4, 4), ("lat_0", "lat_1", "lon_0", "lon_1"))
    placed = (
        P(LAT_LON, None),
        P(LAT_LON, None),
        P(LAT_LON),
        P(LAT_LON),
        P(),
        P(),
        P(),
        P(),
        P(LAT_LON, None, None),
    )
    return jax.shard_map(
        local,
        mesh=finer,
        in_specs=placed,
        out_specs=(P(LAT_LON, None, None), P(), P(), P(), P()),
        check_vma=False,
    )
```

profile of v0, /device:TPU:1, one launch (start us, length us, event | category | flops | bytes accessed | tf_op | source)
XLA Modules:
  0.0 191.7 jit_solution(17764597889850920634)
XLA Ops:
  3.5 6.2 %scatter_custom_fusion = s32[3072]{0:T(1024)S(1)} fusion(s32[1536]{0:T(1024)S(1)} %fusion.37, s32[1536]{0:T(1024)S(1)} %fusion.36, s32[]{:T(128)} %constant.23.clone.1), kind=kCustom, calls=%fused_computation.91 | custom fusion | bytes 12292 | tf_op jit(solution)/shard_map/scatter | solution.py:150
  10.4 11.5 %all-to-all-start = ((s32[128,1,24]{2,1,0:T(1,128)}), s32[128,1,24]{2,1,0:T(1,128)S(1)}, u32[]{:S(2)}, u32[]{:S(2)}) async-start(s32[128,1,24]{2,1,0:T(1,128)} %bitcast.5), calls=%async_computation | async-start | bytes 131072 | tf_op jit(solution)/shard_map/all_to_all | solution.py:151
  22.8 1.8 reduce.11
  25.4 5.7 %scatter_custom_fusion.1 = bf16[3072,128]{1,0:T(8,128)(2,1)} fusion(s32[1536]{0:T(1024)S(1)} %fusion.37, bf16[1536,128]{1,0:T(8,128)(2,1)} %param.9, bf16[]{:T(256)} %constant.28.clone.1), kind=kCustom, calls=%fused_computation.68 | custom fusion | bytes 786944 | tf_op jit(solution)/shard_map/scatter | solution.py:158
  31.4 6.3 %all-to-all-start.3 = ((bf16[16,2,3072]{2,1,0:T(2,128)(2,1)}), bf16[16,2,3072]{2,1,0:T(2,128)(2,1)S(1)}, u32[]{:S(2)}, u32[]{:S(2)}) async-start(bf16[16,2,3072]{2,1,0:T(2,128)(2,1)} %reshape.281), calls=%async_computation.3 | async-start | bytes 393216 | tf_op jit(solution)/shard_map/all_to_all | solution.py:185
  37.9 6.9 %all-to-all-done.3 = bf16[16,2,3072]{2,1,0:T(2,128)(2,1)S(1)} async-done(((bf16[16,2,3072]{2,1,0:T(2,128)(2,1)}), bf16[16,2,3072]{2,1,0:T(2,128)(2,1)S(1)}, u32[]{:S(2)}, u32[]{:S(2)}) %all-to-all-start.3) | async-done | bytes 196640 | tf_op jit(solution)/shard_map/all_to_all | solution.py:185
  44.9 7.8 %all-to-all-start.1 = ((bf16[128,24,128]{2,1,0:T(8,128)(2,1)}), bf16[128,24,128]{2,1,0:T(8,128)(2,1)S(1)}, u32[]{:S(2)}, u32[]{:S(2)}) async-start(bf16[128,24,128]{2,1,0:T(8,128)(2,1)} %bitcast.6), calls=%async_computation.1 | async-start | bytes 1572864 | tf_op jit(solution)/shard_map/all_to_all | solution.py:160
  55.5 4.0 %collective-permute-done.5 = bf16[1,24,256]{2,1,0:T(8,128)(2,1)S(1)} collective-permute-done((bf16[1,24,256]{2,1,0:T(8,128)(2,1)S(1)}, bf16[1,24,256]{2,1,0:T(8,128)(2,1)S(1)}, u32[]{:S(2)}, u32[]{:S(2)}) %collective-permute-start.5) | collective-permute-done | bytes 12320 | tf_op jit(solution)/shard_map/ppermute | solution.py:25
  60.8 7.1 %collective-permute-start.7 = (bf16[18,1,256]{2,1,0:T(2,128)(2,1)S(1)}, bf16[18,1,256]{2,1,0:T(2,128)(2,1)S(1)}, u32[]{:S(2)}, u32[]{:S(2)}) collective-permute-start(bf16[18,1,256]{2,1,0:T(2,128)(2,1)S(1)} %get-tuple-element.21), channel_id=1, source_target_pairs={{1,0},{2,1},{3,2},{4,3},{5,4},{6,5},{7,6},{8,7},{9,8},{10,9},{11,1... | collective-permute-start | bytes 27656 | tf_op jit(solution)/shard_map/ppermute | solution.py:25
  69.7 11.1 %gather_fusion = bf16[3072,256]{1,0:T(8,128)(2,1)S(1)} fusion(bf16[385,256]{1,0:T(8,128)(2,1)S(1)} %concatenate.22, s32[3072]{0:T(1024)S(1)} %broadcast_clamp_fusion), kind=kCustom, calls=%fused_computation | custom fusion | bytes 3158016 | tf_op jit(solution)/shard_map/gather | solution.py:205
  80.8 2.3 %fusion.44 = f32[3072,256]{1,0:T(8,128)} fusion(bf16[3072,256]{1,0:T(8,128)(2,1)S(1)} %gather_fusion, bf16[256,256]{1,0:T(8,128)(2,1)S(1)} %copy-done), kind=kOutput, calls=%fused_computation.107 | convolution fusion | flops 402653184 | bytes 4849664 | tf_op jit(solution)/shard_map/dot_general | solution.py:101
  83.1 5.0 %convert_reduce_fusion = (f32[256]{0:T(256)S(1)}, bf16[3072,256]{1,0:T(8,128)(2,1)}, f32[3072,256]{1,0:T(8,128)S(1)}) fusion(f32[3072,256]{1,0:T(8,128)} %fusion.44, f32[256]{0:T(256)S(1)} %copy-done.7, bf16[3072,128]{1,0:T(8,128)(2,1)S(1)} %bitcast.77, bf16[128,256]{1,0:T(8,128)(2,1)S(1)} %copy-done.6), kind=kOutput, calls=%fused_computation.16 | convolution fusion | flops 219414272 | bytes 8718336 | tf_op jit(solution)/shard_map/dot_general | solution.py:92
  89.8 2.8 %fusion = f32[3072,256]{1,0:T(8,128)} fusion(bf16[256,256]{1,0:T(8,128)(2,1)S(1)} %copy-done, f32[3072,256]{1,0:T(8,128)S(1)} %get-tuple-element.31), kind=kOutput, calls=%fused_computation.8 | convolution fusion | flops 411303936 | bytes 6422528 | tf_op jit(solution)/shard_map/dot_general | solution.py:94
  92.6 17.6 %scatter_custom_fusion.2 = f32[385,256]{1,0:T(8,128)S(1)} fusion(s32[3072]{0:T(1024)S(1)} %reshape.253, f32[3072,256]{1,0:T(8,128)} %fusion, f32[]{:T(128)} %constant.22.clone.1), kind=kCustom, calls=%fused_computation.72 | custom fusion | flops 786432 | bytes 394752 | tf_op jit(solution)/shard_map/scatter-add | solution.py:169
  112.6 3.1 %convolution_bitcast_fusion = f32[32,2,8,128]{3,2,1,0:T(8,128)S(1)} fusion(bf16[3072,256]{1,0:T(8,128)(2,1)S(1)} %gather_fusion, f32[3072,256]{1,0:T(8,128)} %copy-done.8), kind=kOutput, calls=%fused_computation.27 | convolution fusion | flops 409731072 | bytes 4980736 | tf_op jit(solution)/shard_map/dot_general | solution.py:100
  115.8 7.2 %collective-permute-start.3 = (f32[18,1,256]{2,1,0:T(1,128)S(1)}, f32[18,1,256]{2,1,0:T(1,128)S(1)}, u32[]{:S(2)}, u32[]{:S(2)}) collective-permute-start(f32[18,1,256]{2,1,0:T(1,128)S(1)} %get-tuple-element.17), channel_id=1, source_target_pairs={{1,0},{2,1},{3,2},{4,3},{5,4},{6,5},{7,6},{8,7},{9,8},{10,9},{11,1... | collective-permute-start | bytes 55304 | tf_op jit(solution)/shard_map/ppermute | solution.py:25
  125.3 9.0 %all_to_all.66 = f32[4,32,788]{2,1,0:T(8,128)S(1)} all-to-all(f32[4,32,788]{2,1,0:T(8,128)S(1)} %copy.27), channel_id=1, replica_groups=mesh['lat_0'=4,'lat_1'=2,'lon_0'=4,'lon_1'=4] {'lon_1'}, dimensions={0} | all-to-all | bytes 806912 | tf_op jit(solution)/shard_map/all_to_all | solution.py:64
  134.4 19.0 %all_to_all.67 = f32[32,1,788]{2,1,0:T(1,128)S(1)} all-to-all(f32[32,1,788]{2,1,0:T(1,128)S(1)} %all_to_all.54), channel_id=1, replica_groups=mesh['lat_0'=4,'lat_1'=2,'lon_0'=4,'lon_1'=4] {'lat_0','lat_1','lon_0'}, dimensions={0} | all-to-all | bytes 201728 | tf_op jit(solution)/shard_map/all_to_all | solution.py:72
  154.2 4.0 %all-to-all-start.6 = ((f32[32,1,788]{2,1,0:T(1,128)}), f32[32,1,788]{2,1,0:T(1,128)S(1)}, u32[]{:S(2)}, u32[]{:S(2)}) async-start(f32[32,1,788]{2,1,0:T(1,128)} %broadcast_in_dim.20), calls=%async_computation.6 | async-start | bytes 229376 | tf_op jit(solution)/shard_map/all_to_all | solution.py:39
  159.2 6.5 %all-to-all-done.6 = f32[32,1,788]{2,1,0:T(1,128)S(1)} async-done(((f32[32,1,788]{2,1,0:T(1,128)}), f32[32,1,788]{2,1,0:T(1,128)S(1)}, u32[]{:S(2)}, u32[]{:S(2)}) %all-to-all-start.6) | async-done | bytes 100896 | tf_op jit(solution)/shard_map/all_to_all | solution.py:39
  165.7 3.5 %all-to-all-start.2 = ((bf16[16,24,256]{2,1,0:T(8,128)(2,1)}), bf16[16,24,256]{2,1,0:T(8,128)(2,1)S(1)}, u32[]{:S(2)}, u32[]{:S(2)}) async-start(bf16[16,24,256]{2,1,0:T(8,128)(2,1)} %add_convert_fusion), calls=%async_computation.2 | async-start | bytes 393216 | tf_op jit(solution)/shard_map/all_to_all | solution.py:181
  169.2 6.9 %all-to-all-done.2 = bf16[16,24,256]{2,1,0:T(8,128)(2,1)S(1)} async-done(((bf16[16,24,256]{2,1,0:T(8,128)(2,1)}), bf16[16,24,256]{2,1,0:T(8,128)(2,1)S(1)}, u32[]{:S(2)}, u32[]{:S(2)}) %all-to-all-start.2) | async-done | bytes 196640 | tf_op jit(solution)/shard_map/all_to_all | solution.py:181
  176.9 3.5 %all-to-all-start.7 = ((f32[4,32,788]{2,1,0:T(8,128)}), f32[4,32,788]{2,1,0:T(8,128)S(1)}, u32[]{:S(2)}, u32[]{:S(2)}) async-start(f32[4,32,788]{2,1,0:T(8,128)} %broadcast_in_dim.41), calls=%async_computation.7 | async-start | bytes 917504 | tf_op jit(solution)/shard_map/all_to_all | solution.py:39
  180.4 6.7 %all-to-all-done.7 = f32[4,32,788]{2,1,0:T(8,128)S(1)} async-done(((f32[4,32,788]{2,1,0:T(8,128)}), f32[4,32,788]{2,1,0:T(8,128)S(1)}, u32[]{:S(2)}, u32[]{:S(2)}) %all-to-all-start.7) | async-done | bytes 403488 | tf_op jit(solution)/shard_map/all_to_all | solution.py:39
  (98 shorter events, 24.2 us)
Async XLA Ops:
  0.6 80.2 %copy-start = (bf16[256,256]{1,0:T(8,128)(2,1)S(1)}, bf16[256,256]{1,0:T(8,128)(2,1)}, u32[]{:S(2)}) copy-start(bf16[256,256]{1,0:T(8,128)(2,1)} %param.15) | copy-start | bytes 393220
  0.6 2.8 %copy-start.3 = (s32[1536,1]{0,1:T(1,128)S(1)}, s32[1536,1]{0,1:T(1,128)}, u32[]{:S(2)}) copy-start(s32[1536,1]{0,1:T(1,128)} %param.10) | copy-start | bytes 18436
  0.7 2.8 %copy-start.4 = (s32[1536]{0:T(1024)S(1)}, s32[1536]{0:T(1024)}, u32[]{:S(2)}) copy-start(s32[1536]{0:T(1024)} %param.11) | copy-start | bytes 18436
  0.7 21.3 %copy-start.2 = (bf16[1,384,256]{2,1,0:T(8,128)(2,1)S(1)}, bf16[1,384,256]{2,1,0:T(8,128)(2,1)}, u32[]{:S(2)}) copy-start(bf16[1,384,256]{2,1,0:T(8,128)(2,1)} %param.17) | copy-start | bytes 589828
  2.7 35.1 %copy-start.5 = (f32[9,256]{1,0:T(8,128)S(1)}, f32[9,256]{1,0:T(8,128)}, u32[]{:S(2)}) copy-start(f32[9,256]{1,0:T(8,128)} %param.16) | copy-start | bytes 27652
  10.4 21.0 %all-to-all-start = ((s32[128,1,24]{2,1,0:T(1,128)}), s32[128,1,24]{2,1,0:T(1,128)S(1)}, u32[]{:S(2)}, u32[]{:S(2)}) async-start(s32[128,1,24]{2,1,0:T(1,128)} %bitcast.5), calls=%async_computation | async-start | bytes 131072 | tf_op jit(solution)/shard_map/all_to_all | solution.py:151
  31.4 13.4 %all-to-all-start.3 = ((bf16[16,2,3072]{2,1,0:T(2,128)(2,1)}), bf16[16,2,3072]{2,1,0:T(2,128)(2,1)S(1)}, u32[]{:S(2)}, u32[]{:S(2)}) async-start(bf16[16,2,3072]{2,1,0:T(2,128)(2,1)} %reshape.281), calls=%async_computation.3 | async-start | bytes 393216 | tf_op jit(solution)/shard_map/all_to_all | solution.py:185
  44.9 38.3 %all-to-all-start.1 = ((bf16[128,24,128]{2,1,0:T(8,128)(2,1)}), bf16[128,24,128]{2,1,0:T(8,128)(2,1)S(1)}, u32[]{:S(2)}, u32[]{:S(2)}) async-start(bf16[128,24,128]{2,1,0:T(8,128)(2,1)} %bitcast.6), calls=%async_computation.1 | async-start | bytes 1572864 | tf_op jit(solution)/shard_map/all_to_all | solution.py:160
  52.9 2.6 %collective-permute-start.4 = (bf16[1,24,256]{2,1,0:T(8,128)(2,1)S(1)}, bf16[1,24,256]{2,1,0:T(8,128)(2,1)S(1)}, u32[]{:S(2)}, u32[]{:S(2)}) collective-permute-start(bf16[1,24,256]{2,1,0:T(8,128)(2,1)S(1)} %slice_bitcast_fusion.2), channel_id=1, source_target_pairs={{0,16},{16,32},{32,48},{48,64},{64,80},{80,96},{96,112},{112,0},{1... | collective-permute-start | bytes 36872 | tf_op jit(solution)/shard_map/ppermute | solution.py:24
  54.7 4.9 %collective-permute-start.5 = (bf16[1,24,256]{2,1,0:T(8,128)(2,1)S(1)}, bf16[1,24,256]{2,1,0:T(8,128)(2,1)S(1)}, u32[]{:S(2)}, u32[]{:S(2)}) collective-permute-start(bf16[1,24,256]{2,1,0:T(8,128)(2,1)S(1)} %copy.33), channel_id=1, source_target_pairs={{16,0},{32,16},{48,32},{64,48},{80,64},{96,80},{112,96},{0,112},{1... | collective-permute-start | bytes 36872 | tf_op jit(solution)/shard_map/ppermute | solution.py:25
  59.6 9.7 %collective-permute-start.6 = (bf16[18,1,256]{2,1,0:T(2,128)(2,1)S(1)}, bf16[18,1,256]{2,1,0:T(2,128)(2,1)S(1)}, u32[]{:S(2)}, u32[]{:S(2)}) collective-permute-start(bf16[18,1,256]{2,1,0:T(2,128)(2,1)S(1)} %get-tuple-element.20), channel_id=1, source_target_pairs={{0,1},{1,2},{2,3},{3,4},{4,5},{5,6},{6,7},{7,8},{8,9},{9,10},{10,1... | collective-permute-start | bytes 27656 | tf_op jit(solution)/shard_map/ppermute | solution.py:24
  60.8 8.5 %collective-permute-start.7 = (bf16[18,1,256]{2,1,0:T(2,128)(2,1)S(1)}, bf16[18,1,256]{2,1,0:T(2,128)(2,1)S(1)}, u32[]{:S(2)}, u32[]{:S(2)}) collective-permute-start(bf16[18,1,256]{2,1,0:T(2,128)(2,1)S(1)} %get-tuple-element.21), channel_id=1, source_target_pairs={{1,0},{2,1},{3,2},{4,3},{5,4},{6,5},{7,6},{8,7},{9,8},{10,9},{11,1... | collective-permute-start | bytes 27656 | tf_op jit(solution)/shard_map/ppermute | solution.py:25
  80.8 2.3 %copy-start.6 = (bf16[128,256]{1,0:T(8,128)(2,1)S(1)}, bf16[128,256]{1,0:T(8,128)(2,1)}, u32[]{:S(2)}) copy-start(bf16[128,256]{1,0:T(8,128)(2,1)} %param.13) | copy-start | bytes 196612
  80.8 2.3 %copy-start.7 = (f32[256]{0:T(256)S(1)}, f32[256]{0:T(256)}, u32[]{:S(2)}) copy-start(f32[256]{0:T(256)} %param.14) | copy-start | bytes 3076
  88.1 1.7 copy-start.8
  110.2 5.5 %collective-permute-start = (f32[1,24,256]{2,1,0:T(8,128)S(1)}, f32[1,24,256]{2,1,0:T(8,128)S(1)}, u32[]{:S(2)}, u32[]{:S(2)}) collective-permute-start(f32[1,24,256]{2,1,0:T(8,128)S(1)} %get-tuple-element.18), channel_id=1, source_target_pairs={{0,16},{16,32},{32,48},{48,64},{64,80},{80,96},{96,112},{112,0},{1... | collective-permute-start | bytes 73736 | tf_op jit(solution)/shard_map/ppermute | solution.py:24
  111.5 11.5 %copy-start.1 = (bf16[3072,256]{1,0:T(8,128)(2,1)S(1)}, bf16[3072,256]{1,0:T(8,128)(2,1)}, u32[]{:S(2)}) copy-start(bf16[3072,256]{1,0:T(8,128)(2,1)} %get-tuple-element.15) | copy-start | bytes 4718596
  111.5 4.2 %collective-permute-start.1 = (f32[1,24,256]{2,1,0:T(8,128)S(1)}, f32[1,24,256]{2,1,0:T(8,128)S(1)}, u32[]{:S(2)}, u32[]{:S(2)}) collective-permute-start(f32[1,24,256]{2,1,0:T(8,128)S(1)} %get-tuple-element.19), channel_id=1, source_target_pairs={{16,0},{32,16},{48,32},{64,48},{80,64},{96,80},{112,96},{0,112},{1... | collective-permute-start | bytes 73736 | tf_op jit(solution)/shard_map/ppermute | solution.py:25
  115.8 8.4 %collective-permute-start.2 = (f32[18,1,256]{2,1,0:T(1,128)S(1)}, f32[18,1,256]{2,1,0:T(1,128)S(1)}, u32[]{:S(2)}, u32[]{:S(2)}) collective-permute-start(f32[18,1,256]{2,1,0:T(1,128)S(1)} %get-tuple-element.16), channel_id=1, source_target_pairs={{0,1},{1,2},{2,3},{3,4},{4,5},{5,6},{6,7},{7,8},{8,9},{9,10},{10,1... | collective-permute-start | bytes 55304 | tf_op jit(solution)/shard_map/ppermute | solution.py:24
  115.8 8.3 %collective-permute-start.3 = (f32[18,1,256]{2,1,0:T(1,128)S(1)}, f32[18,1,256]{2,1,0:T(1,128)S(1)}, u32[]{:S(2)}, u32[]{:S(2)}) collective-permute-start(f32[18,1,256]{2,1,0:T(1,128)S(1)} %get-tuple-element.17), channel_id=1, source_target_pairs={{1,0},{2,1},{3,2},{4,3},{5,4},{6,5},{7,6},{8,7},{9,8},{10,9},{11,1... | collective-permute-start | bytes 55304 | tf_op jit(solution)/shard_map/ppermute | solution.py:25
  154.2 11.5 %all-to-all-start.6 = ((f32[32,1,788]{2,1,0:T(1,128)}), f32[32,1,788]{2,1,0:T(1,128)S(1)}, u32[]{:S(2)}, u32[]{:S(2)}) async-start(f32[32,1,788]{2,1,0:T(1,128)} %broadcast_in_dim.20), calls=%async_computation.6 | async-start | bytes 229376 | tf_op jit(solution)/shard_map/all_to_all | solution.py:39
  165.7 10.4 %all-to-all-start.2 = ((bf16[16,24,256]{2,1,0:T(8,128)(2,1)}), bf16[16,24,256]{2,1,0:T(8,128)(2,1)S(1)}, u32[]{:S(2)}, u32[]{:S(2)}) async-start(bf16[16,24,256]{2,1,0:T(8,128)(2,1)} %add_convert_fusion), calls=%async_computation.2 | async-start | bytes 393216 | tf_op jit(solution)/shard_map/all_to_all | solution.py:181
  176.9 10.2 %all-to-all-start.7 = ((f32[4,32,788]{2,1,0:T(8,128)}), f32[4,32,788]{2,1,0:T(8,128)S(1)}, u32[]{:S(2)}, u32[]{:S(2)}) async-start(f32[4,32,788]{2,1,0:T(8,128)} %broadcast_in_dim.41), calls=%async_computation.7 | async-start | bytes 917504 | tf_op jit(solution)/shard_map/all_to_all | solution.py:39
where the time goes:
time: 193 us; the launch traced here: 192 us
  starting transfers between devices  56.3 us (29%)
  local copies, waits for them, and re-layouts  35.2 us (18%)
  waiting for transfers between devices  32.6 us (17%)
  blocking collectives  28 us (15%)
  other arithmetic  24.1 us (12%)
  matrix products  13.6 us (7%)
    all_to_all x1, blocking collectives, summed_rows(): lax.all_to_all(nearer, far, split_axis=0, concat_axis=0, tiled=True)  19 us
    scatter-add x1, other arithmetic, local(): jax.ops.segment_sum(arrived_enc.astype(jnp.float32), got_cells, num_segme...  17.6 us
    ppermute x4, starting transfers between devices, extended(): after = lax.ppermute(first, axis, down)  15.3 us
    all_to_all x2, waiting for transfers between devices, copy_for_each(): lax.all_to_all(jnp.broadcast_to(shard[None], (count, *shard.shape)), axis...  13.2 us
    all_to_all x1, starting transfers between devices, local(): lax.all_to_all(sent_cells.reshape(devices_all, capacity), LAT_LON, split_...  11.5 us
    gather x1, local copies, waits for them, and re-layouts, local(): upstream = adjoint_rows[got_cells]  11.1 us
    all_to_all x1, blocking collectives, sum_at_owner(): lax.all_to_all(in_blocks(shard, dim, count), axis, 0, 0, tiled=True)  8.96 us
    all_to_all x1, starting transfers between devices, local(): lax.all_to_all(outgoing.reshape(devices_all, capacity, width), LAT_LON, s...  7.81 us
  transfers between devices with their start and end apart: 14, of which 8 were waited for; matrix products, arithmetic and copies ran while one was open for 15% of the time, Pallas kernels for 0%

commit v1 on v0

v1 whole, which is shorter than its diff:
```python
import functools
import math

import jax
import jax.numpy as jnp
from jax import lax
from jax.experimental import pallas as pl
from jax.experimental.pallas import tpu as pltpu
from jax.sharding import PartitionSpec as P

MESH = pl.DeviceIdType.MESH
F32, BF16, I32 = jnp.float32, jnp.bfloat16, jnp.int32
NT = (((1,), (1,)), ((), ()))
TAPS = [(a, b) for a in (-1, 0, 1) for b in (-1, 0, 1)]

N_DEV, N_GRP, GRP = 128, 8, 16
OBS, FEAT, HID, CH = 1536, 128, 256, 256
CAP = 24
SLOTS = GRP * CAP
TLAT, TLON = 16, 24
CELLS = TLAT * TLON
GLON = 384
CHUNKS_IN, CHUNKS_OUT, CHUNKS_SMALL = 32, 64, 3
SCALE = 1.0 / math.sqrt(OBS * N_DEV)
C0, C1 = math.sqrt(2.0 / math.pi), 0.044715


def iota(shape, dim):
    return lax.broadcasted_iota(I32, shape, dim)


def mm(a, b):
    return jnp.dot(a, b, preferred_element_type=F32)


def mm_nt(a, b):
    return lax.dot_general(a, b, NT, preferred_element_type=F32)


def kernel(
    obs_ref, owner_ref, cell_ref, count_ref, w_in_ref, bias_ref, w_out_ref, taps_ref, cot_ref,
    grid_ref, g_in_ref, g_bias_ref, g_out_ref, g_taps_ref,
    send_rows, recv_rows, send_cells, recv_cells, send_cot, recv_cot, cot_f, dep, send_grid,
    chunks, parts, red, shared, acc_in, acc_out, acc_bias, adj_t, sel_rows,
    row_send, row_recv, cell_send, cell_recv, cot_send, cot_recv, fwd_send, fwd_recv,
    part_send, part_recv, share_send, share_recv, halo_send, halo_recv, grid_send, grid_recv,
):
    lat, lon = lax.axis_index("lat"), lax.axis_index("lon")
    z, c, x, y = lax.div(lat, 2), lax.rem(lat, 2), lax.div(lon, 4), lax.rem(lon, 4)
    me = lat * GRP + lon
    lons = [lax.rem(x + j // 4, 4) * 4 + lax.rem(y + j % 4, 4) for j in range(GRP)]

    def lat_of(g):
        return lax.rem(z + lax.div(g, 2), 4) * 2 + lax.rem(c + lax.rem(g, 2), 2)

    def each_peer(fn):
        def body(g, carry):
            to_lat = lat_of(g)
            for j in range(GRP):
                if j:
                    fn(g, j, to_lat, lons[j])
                else:
                    pl.when(g > 0)(lambda: fn(g, 0, to_lat, lons[0]))
            return carry

        lax.fori_loop(0, N_GRP, body, 0)

    def remote(src, dst, send, recv, to_lat, to_lon):
        return pltpu.make_async_remote_copy(
            src_ref=src, dst_ref=dst, send_sem=send, recv_sem=recv,
            device_id=(to_lat, to_lon), device_id_type=MESH,
        )

    def wait_sent(ref, sem):
        remote(ref, ref, sem, sem, lat, lon).wait_send()

    def wait_got(ref, sem):
        remote(ref, ref, sem, sem, lat, lon).wait_recv()

    dep[...] = jnp.zeros_like(dep)
    recv_cot[0] = jnp.zeros(recv_cot.shape[1:], BF16)
    recv_cot[TLAT + 1] = jnp.zeros(recv_cot.shape[1:], BF16)

    barrier = pltpu.get_barrier_semaphore()

    def greet(g, j, to_lat, to_lon):
        pl.semaphore_signal(barrier, inc=1, device_id=(to_lat, to_lon), device_id_type=MESH)

    each_peer(greet)

    owner = owner_ref[...]
    valid = iota((1, OBS), 1) < count_ref[0]
    o_lat, o_lon = owner // GRP, owner % GRP
    rel = (
        (((o_lat // 2) - z + 4) % 4) * 32
        + ((o_lat % 2) - c + 2) % 2 * 16
        + ((o_lon // 4) - x + 4) % 4 * 4
        + ((o_lon % 4) - y + 4) % 4
    )
    rel = jnp.where(valid, rel, -1)
    upto = jnp.where(iota((256, 256), 0) <= iota((256, 256), 1), 1.0, 0.0).astype(BF16)
    peer_ids = iota((N_DEV, 256), 0)
    carry = jnp.zeros((N_DEV, 1), F32)
    ranks = []
    for i in range(OBS // 256):
        hit = jnp.where(peer_ids == rel[:, i * 256 : (i + 1) * 256], 1.0, 0.0)
        count = mm(hit.astype(BF16), upto) + carry
        ranks.append(jnp.sum(hit * count, axis=0, keepdims=True) - 1.0)
        carry = count[:, 255:256]
    rank = jnp.concatenate(ranks, axis=1).astype(I32)
    key = jnp.where(valid, rel * CAP + rank, -1)

    value = cell_ref[...] + 1
    high = jnp.where(value >= 256, 1.0, 0.0)
    low = value.astype(F32) - 256.0 * high
    cells_high = jnp.zeros((N_DEV, 128), F32)
    cells_low = jnp.zeros((N_DEV, 128), F32)
    for i in range(OBS // 256):
        part = slice(i * 256, (i + 1) * 256)
        hit = jnp.where(peer_ids == rel[:, part], 1.0, 0.0)
        place = jnp.where(iota((128, 256), 0) == rank[:, part], 1.0, 0.0).astype(BF16)
        cells_high += mm_nt((hit * high[:, part]).astype(BF16), place)
        cells_low += mm_nt((hit * low[:, part]).astype(BF16), place)
    cells = (256.0 * cells_high + cells_low).reshape(N_GRP, GRP, 128)
    send_cells[...] = cells
    recv_cells[0, 0:1] = cells[0, 0:1]

    pl.semaphore_wait(barrier, N_DEV - 1)

    def send_cell(g, j, to_lat, to_lon):
        remote(
            send_cells.at[g, pl.ds(j, 1)], recv_cells.at[g, pl.ds(j, 1)],
            cell_send.at[g], cell_recv.at[g], to_lat, to_lon,
        ).start()

    each_peer(send_cell)

    def pack(g, carry):
        total = jnp.zeros((SLOTS, FEAT), F32)
        for i in range(OBS // 256):
            part = slice(i * 256, (i + 1) * 256)
            take = jnp.where(iota((SLOTS, 256), 0) + g * SLOTS == key[:, part], 1.0, 0.0)
            total += mm(take.astype(BF16), obs_ref[part, :])
        send_rows[pl.ds(g * GRP, GRP)] = total.reshape(GRP, CAP, FEAT).astype(BF16)
        to_lat = lat_of(g)
        for j in range(GRP):
            def send_row(j=j):
                remote(
                    send_rows.at[g * GRP + j], recv_rows.at[g * GRP + j],
                    row_send.at[g], row_recv.at[g], to_lat, lons[j],
                ).start()

            if j:
                send_row()
            else:
                pl.when(g > 0)(send_row)
        return carry

    lax.fori_loop(0, N_GRP, pack, 0)
    recv_rows[0] = send_rows[0]

    where_from = iota((GRP * 32, GLON), 0)
    tile, slot = where_from // 32, where_from % 32
    column = jnp.where(
        slot < TLON,
        tile * TLON + slot,
        jnp.where(
            slot == TLON,
            (tile * TLON + GLON - 1) % GLON,
            jnp.where(slot == TLON + 1, (tile * TLON + TLON) % GLON, -1),
        ),
    )
    pick = jnp.where(column == iota((GRP * 32, GLON), 1), 1.0, 0.0).astype(BF16)
    send_cot[...] = mm(pick, cot_ref[...]).reshape(GRP, 32, CH).astype(BF16)
    for j in range(1, GRP):
        remote(
            send_cot.at[lons[j]], recv_cot.at[1 + lon], cot_send, cot_recv, lat, lons[j]
        ).start()
    recv_cot[1 + lon] = send_cot[lon]

    w_in_t = w_in_ref[...].astype(F32).T.astype(BF16)
    w_out = w_out_ref[...]
    w_out_t = w_out.astype(F32).T.astype(BF16)
    bias_t = jnp.broadcast_to(bias_ref[...], (128, HID)).T[:, 0:1]
    for g in range(N_GRP):
        got = recv_cells.at[g] if g else recv_cells.at[0, pl.ds(0, GRP - 1)]
        wait_got(got, cell_recv.at[g])
    codes = recv_cells[...].reshape(N_DEV, 128)
    high = jnp.where(codes >= 256.0, 1.0, 0.0)
    spread = jnp.where(iota((128, SLOTS), 0) == iota((128, SLOTS), 1) % CAP, 1.0, 0.0).astype(BF16)
    codes = 256.0 * mm(high.astype(BF16), spread) + mm((codes - 256.0 * high).astype(BF16), spread)
    own = iota((GRP, SLOTS), 0) == iota((GRP, SLOTS), 1) // CAP
    for g in range(N_GRP):
        mine = jnp.where(own, codes[g * GRP : (g + 1) * GRP], 0.0)
        sel_rows[g] = jnp.sum(mine, axis=0, keepdims=True).astype(I32) - 1

    wait_got(recv_cot.at[pl.ds(0, GRP - 1)], cot_recv)

    @pl.when(lat > 0)
    def _():
        remote(
            recv_cot.at[1], recv_cot.at[TLAT + 1], fwd_send.at[0], fwd_recv.at[0], lat - 1, lon
        ).start()

    @pl.when(lat < N_GRP - 1)
    def _():
        remote(
            recv_cot.at[TLAT], recv_cot.at[0], fwd_send.at[1], fwd_recv.at[1], lat + 1, lon
        ).start()

    @pl.when(lat < N_GRP - 1)
    def _():
        wait_got(recv_cot.at[TLAT + 1], fwd_recv.at[0])

    @pl.when(lat > 0)
    def _():
        wait_got(recv_cot.at[0], fwd_recv.at[1])

    cot_all = recv_cot[...].astype(F32)
    cot_f[:, 8:32, :] = cot_all[:, 0:TLON]
    cot_f[:, 7:8, :] = cot_all[:, TLON : TLON + 1]
    cot_f[:, 32:33, :] = cot_all[:, TLON + 1 : TLON + 2]

    def adjoint_row(r, carry):
        total = jnp.zeros((TLON, CH), F32)
        for k, (a, b) in enumerate(TAPS):
            total += taps_ref[k : k + 1, :] * cot_f[r + 1 - a, 8 - b : 8 - b + TLON, :]
        send_grid[r] = (SCALE * total).astype(BF16)
        return carry

    lax.fori_loop(0, TLAT, adjoint_row, 0)
    adj_t[...] = send_grid[...].astype(F32).reshape(CELLS, CH).T.astype(BF16)

    acc_in[...] = jnp.zeros_like(acc_in)
    acc_out[...] = jnp.zeros_like(acc_out)
    acc_bias[...] = jnp.zeros_like(acc_bias)

    def work(g):
        rows = recv_rows[pl.ds(g * GRP, GRP)].astype(F32).reshape(SLOTS, FEAT).astype(BF16)
        before = mm_nt(w_in_t, rows) + bias_t
        square = before * before
        t = jnp.tanh(C0 * before * (1.0 + C1 * square))
        half = 0.5 * (1.0 + t)
        slope = half + 0.5 * before * (1.0 - t * t) * (C0 * (1.0 + 3.0 * C1 * square))
        hidden = (before * half).astype(BF16)
        encoded = mm(w_out_t, hidden).astype(BF16)
        place = jnp.where(iota((CELLS, SLOTS), 0) == sel_rows[g], 1.0, 0.0).astype(BF16)
        add = mm_nt(place, encoded).reshape(TLAT, TLON, CH)
        dep[1 : 1 + TLAT, 8 : 8 + TLON, :] += add
        up = mm(adj_t[...], place).astype(BF16)
        pre = (mm(w_out, up) * slope).astype(BF16)
        acc_out[...] += mm_nt(hidden, up)
        acc_in[...] += mm(pre, rows)
        pre = pre.astype(F32)
        acc_bias[...] += pre[:, 0:128] + pre[:, 128:256] + pre[:, 256:384]

    for g in range(N_GRP):
        got = recv_rows.at[pl.ds(g * GRP, GRP if g else GRP - 1)]
        wait_got(got, row_recv.at[g])
        work(g)

    north, south = lat > 0, lat < N_GRP - 1
    west, east = lax.rem(lon + 15, GRP), lax.rem(lon + 1, GRP)
    core = (1, TLAT)
    first, last = (1, 1), (TLAT, 1)
    above, below = (0, 1), (TLAT + 1, 1)
    wide, left, right = (8, TLON), (8, 1), (8 + TLON - 1, 1)
    before_left, after_right = (7, 1), (8 + TLON, 1)
    halos = [
        (None, lat, west, core, left, core, after_right),
        (None, lat, east, core, right, core, before_left),
        (north, lat - 1, lon, first, wide, below, wide),
        (south, lat + 1, lon, last, wide, above, wide),
        (north, lat - 1, west, first, left, below, after_right),
        (north, lat - 1, east, first, right, below, before_left),
        (south, lat + 1, west, last, left, above, after_right),
        (south, lat + 1, east, last, right, above, before_left),
    ]
    comes = [None, None, south, north, south, south, north, north]

    def at(rows, columns):
        return dep.at[pl.ds(*rows), pl.ds(*columns), :]

    for i, (there, to_lat, to_lon, sr, sc, dr, dc) in enumerate(halos):
        def send_halo(i=i, to_lat=to_lat, to_lon=to_lon, sr=sr, sc=sc, dr=dr, dc=dc):
            remote(
                at(sr, sc), at(dr, dc), halo_send.at[i], halo_recv.at[i], to_lat, to_lon
            ).start()

        send_halo() if there is None else pl.when(there)(send_halo)

    def taps_row(r, totals):
        mine = dep[r + 1, 8 : 8 + TLON, :]
        return tuple(
            total + mine * cot_f[r + 1 - a, 8 - b : 8 - b + TLON, :]
            for total, (a, b) in zip(totals, TAPS)
        )

    totals = lax.fori_loop(0, TLAT, taps_row, (jnp.zeros((TLON, CH), F32),) * 9)
    small = [SCALE * jnp.sum(t, axis=0, keepdims=True) for t in totals]
    small.append(jnp.sum(acc_bias[...].T, axis=0, keepdims=True))
    small = [h for s in small for h in (s[:, :128], s[:, 128:])]
    small = jnp.concatenate(small + [jnp.zeros((4, 128), F32)], axis=0)
    small_high = small.astype(BF16)
    small_low = (small - small_high.astype(F32)).astype(BF16)
    chunks[0:32] = acc_in[...].reshape(32, 8, 128).astype(BF16)
    chunks[32:64] = acc_out[:, :128].reshape(32, 8, 128).astype(BF16)
    chunks[64:96] = acc_out[:, 128:].reshape(32, 8, 128).astype(BF16)
    chunks[96:99] = small_high.astype(F32).reshape(3, 8, 128).astype(BF16)
    chunks[99:102] = small_low.astype(F32).reshape(3, 8, 128).astype(BF16)
    chunks[102:128] = jnp.zeros((26, 8, 128), BF16)

    def send_part(g, j, to_lat, to_lon):
        remote(
            chunks.at[to_lat * GRP + to_lon], parts.at[g * GRP + j],
            part_send.at[g], part_recv.at[g], to_lat, to_lon,
        ).start()

    each_peer(send_part)
    parts[0] = chunks[me]

    for i, there in enumerate(comes):
        _, _, _, _, _, dr, dc = halos[i]
        def got_halo(i=i, dr=dr, dc=dc):
            wait_got(at(dr, dc), halo_recv.at[i])

        got_halo() if there is None else pl.when(there)(got_halo)

    def grid_row(r, carry):
        total = jnp.zeros((TLON, CH), F32)
        for k, (a, b) in enumerate(TAPS):
            total += taps_ref[k : k + 1, :] * dep[r + 1 + a, 8 + b : 8 + b + TLON, :]
        send_grid[r] = total.astype(BF16)
        return carry

    lax.fori_loop(0, TLAT, grid_row, 0)
    for j in range(1, GRP):
        remote(
            send_grid.at[lons[j]], grid_ref.at[lon], grid_send, grid_recv, lat, lons[j]
        ).start()
    grid_ref[lon] = send_grid[lon]

    for g in range(N_GRP):
        wait_got(parts.at[pl.ds(g * GRP, GRP if g else GRP - 1)], part_recv.at[g])
    mine = jnp.sum(parts[...].astype(F32), axis=0).astype(BF16)
    red[...] = mine
    shared[me] = mine

    def send_share(g, j, to_lat, to_lon):
        remote(
            red, shared.at[me], share_send.at[g], share_recv.at[g], to_lat, to_lon
        ).start()

    each_peer(send_share)

    for g in range(N_GRP):
        wait_got(shared.at[pl.ds(g * GRP, GRP if g else GRP - 1)], share_recv.at[g])
    whole = shared[...].astype(F32)
    g_in_ref[...] = whole[0:32].reshape(HID, FEAT).T
    g_out_ref[:, :128] = whole[32:64].reshape(HID, 128)
    g_out_ref[:, 128:] = whole[64:96].reshape(HID, 128)
    small = (whole[96:99] + whole[99:102]).reshape(24, 128)
    for k in range(9):
        g_taps_ref[k : k + 1, :128] = small[2 * k : 2 * k + 1]
        g_taps_ref[k : k + 1, 128:] = small[2 * k + 1 : 2 * k + 2]
    g_bias_ref[:, :128] = small[18:19]
    g_bias_ref[:, 128:] = small[19:20]

    wait_got(grid_ref.at[pl.ds(0, GRP - 1)], grid_recv)
    for g in range(N_GRP):
        n = GRP if g else GRP - 1
        wait_sent(send_cells.at[g, pl.ds(0, n)], cell_send.at[g])
        wait_sent(send_rows.at[pl.ds(g * GRP, n)], row_send.at[g])
        wait_sent(chunks.at[pl.ds(g * GRP, n)], part_send.at[g])
        wait_sent(shared.at[pl.ds(g * GRP, n)], share_send.at[g])
    wait_sent(send_cot.at[pl.ds(0, GRP - 1)], cot_send)
    wait_sent(send_grid.at[pl.ds(0, GRP - 1)], grid_send)

    @pl.when(lat > 0)
    def _():
        wait_sent(recv_cot.at[1], fwd_send.at[0])

    @pl.when(lat < N_GRP - 1)
    def _():
        wait_sent(recv_cot.at[TLAT], fwd_send.at[1])

    for i, (there, _, _, sr, sc, _, _) in enumerate(halos):
        def sent_halo(i=i, sr=sr, sc=sc):
            wait_sent(at(sr, sc), halo_send.at[i])

        sent_halo() if there is None else pl.when(there)(sent_halo)


def local(obs, owner, cell, count, w_in, bias, w_out, taps, cot):
    vmem = pl.BlockSpec(memory_space=pltpu.VMEM)
    smem = pl.BlockSpec(memory_space=pltpu.SMEM)
    dma = pltpu.SemaphoreType.DMA
    grid, g_in, g_bias, g_out, g_taps = pl.pallas_call(
        kernel,
        name="encode_step",
        out_shape=(
            jax.ShapeDtypeStruct((GRP, TLON, CH), BF16),
            jax.ShapeDtypeStruct((FEAT, HID), F32),
            jax.ShapeDtypeStruct((1, HID), F32),
            jax.ShapeDtypeStruct((HID, CH), F32),
            jax.ShapeDtypeStruct((9, CH), F32),
        ),
        in_specs=[vmem, vmem, vmem, smem, vmem, vmem, vmem, vmem, vmem],
        out_specs=(vmem,) * 5,
        scratch_shapes=[
            pltpu.VMEM((N_DEV, CAP, FEAT), BF16),
            pltpu.VMEM((N_DEV, CAP, FEAT), BF16),
            pltpu.VMEM((N_GRP, GRP, 128), F32),
            pltpu.VMEM((N_GRP, GRP, 128), F32),
            pltpu.VMEM((GRP, 32, CH), BF16),
            pltpu.VMEM((TLAT + 2, 32, CH), BF16),
            pltpu.VMEM((TLAT + 2, 40, CH), F32),
            pltpu.VMEM((TLAT + 2, 40, CH), F32),
            pltpu.VMEM((TLAT, TLON, CH), BF16),
            pltpu.VMEM((N_DEV, 8, 128), BF16),
            pltpu.VMEM((N_DEV, 8, 128), BF16),
            pltpu.VMEM((8, 128), BF16),
            pltpu.VMEM((N_DEV, 8, 128), BF16),
            pltpu.VMEM((HID, FEAT), F32),
            pltpu.VMEM((HID, CH), F32),
            pltpu.VMEM((HID, 128), F32),
            pltpu.VMEM((CH, CELLS), BF16),
            pltpu.VMEM((N_GRP, 1, SLOTS), I32),
            dma((N_GRP,)), dma((N_GRP,)), dma((N_GRP,)), dma((N_GRP,)),
            dma, dma, dma((2,)), dma((2,)),
            dma((N_GRP,)), dma((N_GRP,)), dma((N_GRP,)), dma((N_GRP,)),
            dma((8,)), dma((8,)), dma, dma,
        ],
        compiler_params=pltpu.CompilerParams(
            collective_id=0, has_side_effects=True, vmem_limit_bytes=50 * 1024 * 1024
        ),
        cost_estimate=pl.CostEstimate(
            flops=4_000_000_000, bytes_accessed=2_000_000, transcendentals=800_000
        ),
    )(
        obs, owner.reshape(1, OBS), cell.reshape(1, OBS), count, w_in, bias.reshape(1, HID),
        w_out, taps, cot.reshape(GLON, CH),
    )
    return (grid.reshape(1, GLON, CH), g_in, g_bias.reshape(HID), g_out, g_taps)


def solution(mesh):
    block = P(("lat", "lon"))
    return jax.shard_map(
        local,
        mesh=mesh,
        in_specs=(block, block, block, block, P(), P(), P(), P(), block),
        out_specs=(block, P(), P(), P(), P()),
        check_vma=False,
    )
```

time: 193 us -> 64.9 us (0.34)
  starting transfers between devices: 56.3 us -> 0 us
  Pallas kernels: 0 us -> 54.9 us
  waiting for transfers between devices: 32.6 us -> 0 us
  blocking collectives: 28 us -> 0 us
  local copies, waits for them, and re-layouts: 35.2 us -> 8.27 us
  other arithmetic: 24.1 us -> 0 us
  matrix products: 13.6 us -> 0 us
    pallas_call x0 -> x1, Pallas kernels: none -> 54.9 us  [local(): pl.pallas_call(kernel, name='encode_step', out_shape=(jax.ShapeDtypeStruc...]
    all_to_all x6 -> x0, starting transfers between devices: 36.6 us -> none  [the longest x1 11.5 us: local(): lax.all_to_all(sent_cells.reshape(devices_all, capacity), LAT_LON, split_...]
    all_to_all x2 -> x0, blocking collectives: 28 us -> none  [the longest x1 19 us: summed_rows(): lax.all_to_all(nearer, far, split_axis=0, concat_axis=0, tiled=True)]
    all_to_all x6 -> x0, waiting for transfers between devices: 27.4 us -> none  [the longest x2 13.2 us: copy_for_each(): lax.all_to_all(jnp.broadcast_to(shard[None], (count, *shard.shape)), axis...]
    ppermute x8 -> x0, starting transfers between devices: 19.7 us -> none  [the longest x4 15.3 us: extended(): after = lax.ppermute(first, axis, down)]
    scatter-add x1 -> x0, other arithmetic: 17.6 us -> none  [local(): jax.ops.segment_sum(arrived_enc.astype(jnp.float32), got_cells, num_segme...]
    dot_general x5 -> x0, matrix products: 13.6 us -> none  [the longest x1 4.97 us: encoder(): jnp.dot(rows, weight_in, preferred_element_type=jnp.float32) + bias_in]
    scatter x2 -> x0, local copies, waits for them, and re-layouts: 11.9 us -> none  [the longest x1 6.19 us: local(): sent_cells.at[slot_index].set(jnp.where(valid_rows, local_cell, cells_tile))]
  transfers between devices with their start and end apart: 14 -> 0, of which waited for: 8 -> 0; matrix products, arithmetic and copies ran while one was open for 15% -> 0% of each run, Pallas kernels for 0% -> 0%
where the time goes in v1:
time: 64.9 us; the launch traced here: 64.6 us
  Pallas kernels  54.9 us (85%)
  local copies, waits for them, and re-layouts  8.27 us (13%)
  between operations  1.33 us (2%)
    pallas_call x1, Pallas kernels, local(): pl.pallas_call(kernel, name='encode_step', out_shape=(jax.ShapeDtypeStruc...  54.9 us
    unnamed x19, local copies, waits for them, and re-layouts  7.56 us

profile of v1, /device:TPU:1, one launch (start us, length us, event | category | flops | bytes accessed | tf_op | source)
XLA Modules:
  0.0 64.6 jit_solution(5455490711894923430)
XLA Ops:
  0.6 0.0 copy-start.4
  1.3 0.0 copy-start.6
  1.3 0.7 %reshape.29.cell_ref = s32[1,1536]{1,0:T(1,128)S(1)} reshape(s32[1536]{0:T(1024)} %param.11) | data formatting | bytes 12288 | tf_op jit(solution)/shard_map/reshape | solution.py:441
  2.0 0.0 copy-done.4
  2.0 0.0 copy-done.6
  2.0 0.0 copy-start
  2.0 1.0 %copy-done = bf16[1536,128]{1,0:T(8,128)(2,1)S(1)} copy-done((bf16[1536,128]{1,0:T(8,128)(2,1)S(1)}, bf16[1536,128]{1,0:T(8,128)(2,1)}, u32[]{:S(2)}) %copy-start) | copy-done | bytes 393240
  3.0 0.0 copy-start.1
  3.0 0.9 %copy-done.1 = bf16[1,384,256]{2,1,0:T(8,128)(2,1)S(1)} copy-done((bf16[1,384,256]{2,1,0:T(8,128)(2,1)S(1)}, bf16[1,384,256]{2,1,0:T(8,128)(2,1)}, u32[]{:S(2)}) %copy-start.1) | copy-done | bytes 196632
  4.0 0.0 copy-start.2
  4.0 0.9 %copy-done.2 = bf16[256,256]{1,0:T(8,128)(2,1)S(1)} copy-done((bf16[256,256]{1,0:T(8,128)(2,1)S(1)}, bf16[256,256]{1,0:T(8,128)(2,1)}, u32[]{:S(2)}) %copy-start.2) | copy-done | bytes 131096
  4.9 0.0 copy-start.3
  4.9 0.8 %copy-done.3 = bf16[128,256]{1,0:T(8,128)(2,1)S(1)} copy-done((bf16[128,256]{1,0:T(8,128)(2,1)S(1)}, bf16[128,256]{1,0:T(8,128)(2,1)}, u32[]{:S(2)}) %copy-start.3) | copy-done | bytes 65560
  5.7 0.0 copy-start.5
  5.7 0.7 %copy-done.5 = s32[1536,1]{0,1:T(1,128)S(1)} copy-done((s32[1536,1]{0,1:T(1,128)S(1)}, s32[1536,1]{0,1:T(1,128)}, u32[]{:S(2)}) %copy-start.5) | copy-done | bytes 6168
  6.4 54.9 %encode_step.1 = (bf16[16,24,256]{2,1,0:T(8,128)(2,1)S(1)}, f32[128,256]{1,0:T(8,128)S(1)}, f32[1,256]{1,0:T(1,128)S(1)}, f32[256,256]{1,0:T(8,128)S(1)}, f32[9,256]{1,0:T(8,128)S(1)}) custom-call(bf16[1536,128]{1,0:T(8,128)(2,1)S(1)} %copy-done, s32[1,1536]{1,0:T(1,128)S(1)} %bitcast.8, s32[1,1536]{1,0:T(1,128)S(1)} %reshape.29.cell_ref, ...), custom_call_target="tpu_custom_call" | custom-call | flops 4000000000 | bytes 2000000 | tf_op jit(solution)/shard_map/encode_step/pallas_call | solution.py:398
  61.3 0.7 %copy.20 = bf16[1,384,256]{2,1,0:T(8,128)(2,1)} copy(bf16[1,384,256]{2,1,0:T(8,128)(2,1)S(1)} %bitcast.5) | data formatting | bytes 393216
  62.0 0.7 %copy.21 = f32[128,256]{1,0:T(8,128)} copy(f32[128,256]{1,0:T(8,128)S(1)} %get-tuple-element.21) | data formatting | bytes 262144
  62.7 0.6 copy.22
  63.2 0.7 %copy.23 = f32[256,256]{1,0:T(8,128)} copy(f32[256,256]{1,0:T(8,128)S(1)} %get-tuple-element.23) | data formatting | bytes 524288
  63.9 0.6 copy.24
Async XLA Ops:
  0.6 1.4 %copy-start.4 = (f32[9,256]{1,0:T(8,128)S(1)}, f32[9,256]{1,0:T(8,128)}, u32[]{:S(2)}) copy-start(f32[9,256]{1,0:T(8,128)} %taps_ref.1) | copy-start | bytes 27652
  1.3 0.7 %copy-start.6 = (f32[256]{0:T(256)S(1)}, f32[256]{0:T(256)}, u32[]{:S(2)}) copy-start(f32[256]{0:T(256)} %param.14) | copy-start | bytes 3076
  2.0 1.0 %copy-start = (bf16[1536,128]{1,0:T(8,128)(2,1)S(1)}, bf16[1536,128]{1,0:T(8,128)(2,1)}, u32[]{:S(2)}) copy-start(bf16[1536,128]{1,0:T(8,128)(2,1)} %obs_ref.1) | copy-start | bytes 1179652
  3.0 0.9 %copy-start.1 = (bf16[1,384,256]{2,1,0:T(8,128)(2,1)S(1)}, bf16[1,384,256]{2,1,0:T(8,128)(2,1)}, u32[]{:S(2)}) copy-start(bf16[1,384,256]{2,1,0:T(8,128)(2,1)} %param.17) | copy-start | bytes 589828
  4.0 0.9 %copy-start.2 = (bf16[256,256]{1,0:T(8,128)(2,1)S(1)}, bf16[256,256]{1,0:T(8,128)(2,1)}, u32[]{:S(2)}) copy-start(bf16[256,256]{1,0:T(8,128)(2,1)} %w_out_ref.1) | copy-start | bytes 393220
  4.9 0.8 %copy-start.3 = (bf16[128,256]{1,0:T(8,128)(2,1)S(1)}, bf16[128,256]{1,0:T(8,128)(2,1)}, u32[]{:S(2)}) copy-start(bf16[128,256]{1,0:T(8,128)(2,1)} %w_in_ref.1) | copy-start | bytes 196612
  5.7 0.7 %copy-start.5 = (s32[1536,1]{0,1:T(1,128)S(1)}, s32[1536,1]{0,1:T(1,128)}, u32[]{:S(2)}) copy-start(s32[1536,1]{0,1:T(1,128)} %param.10) | copy-start | bytes 18436

commit v2 on v1

v2 whole, which is shorter than its diff:
```python
import functools
import math

import jax
import jax.numpy as jnp
from jax import lax
from jax.experimental import pallas as pl
from jax.experimental.pallas import tpu as pltpu
from jax.sharding import PartitionSpec as P

MESH = pl.DeviceIdType.MESH
F32, BF16, I32 = jnp.float32, jnp.bfloat16, jnp.int32
NT = (((1,), (1,)), ((), ()))
TAPS = [(a, b) for a in (-1, 0, 1) for b in (-1, 0, 1)]

N_DEV, N_GRP, GRP = 128, 8, 16
EARLY = 4
STEP = 2
N_STEP = N_GRP // STEP
OBS, FEAT, HID, CH = 1536, 128, 256, 256
CAP = 24
SLOTS = GRP * CAP
TLAT, TLON = 16, 24
CELLS = TLAT * TLON
WIDE = STEP * SLOTS
GLON = 384
CHUNKS_IN, CHUNKS_OUT, CHUNKS_SMALL = 32, 64, 3
SCALE = 1.0 / math.sqrt(OBS * N_DEV)
C0, C1 = math.sqrt(2.0 / math.pi), 0.044715


def iota(shape, dim):
    return lax.broadcasted_iota(I32, shape, dim)


def mm(a, b):
    return jnp.dot(a, b, preferred_element_type=F32)


def mm_nt(a, b):
    return lax.dot_general(a, b, NT, preferred_element_type=F32)


def offset_at(g, j):
    dx, dy = (j // 4 + 1) % 4, (j + 1) % 4
    return (g + 1 - dx - dy) % 4, (g // 4 + 1) % 2, dx, dy


def kernel(
    obs_hbm, owner_hbm, cell_hbm, count_ref, w_in_hbm, bias_hbm, w_out_hbm, taps_hbm, cot_hbm,
    grid_ref, shared,
    obs_ref, owner_ref, cell_ref, w_in_ref, bias_ref, w_out_ref, taps_ref, cot_ref,
    send_rows, recv_rows, send_cells, recv_cells, send_cot, recv_cot, cot_f, cot_s, dep, send_grid,
    chunks, parts, red, acc_in, acc_out, acc_bias, adj_t, places, ups, backs,
    in_sem, own_sem,
    row_send, row_recv, cell_send, cell_recv, cot_send, cot_recv, edge_send, edge_recv,
    part_send, part_recv, share_send, share_recv, halo_send, halo_recv, grid_send, grid_recv,
):
    ins = [
        pltpu.make_async_copy(src, dst, in_sem.at[i])
        for i, (src, dst) in enumerate([
            (owner_hbm, owner_ref), (cell_hbm, cell_ref), (cot_hbm, cot_ref), (obs_hbm, obs_ref),
            (w_in_hbm, w_in_ref), (w_out_hbm, w_out_ref), (bias_hbm, bias_ref), (taps_hbm, taps_ref),
        ])
    ]
    for copy in ins:
        copy.start()

    lat, lon = lax.axis_index("lat"), lax.axis_index("lon")
    z, c, x, y = lax.div(lat, 2), lax.rem(lat, 2), lax.div(lon, 4), lax.rem(lon, 4)
    me = lat * GRP + lon
    up_edge = (lat > 0) & (lon == 0)
    down_edge = (lat < N_GRP - 1) & (lon == GRP - 1)
    zs, cs, xs, ys = ([lax.rem(at + d, n) for d in range(n)] for at, n in ((z, 4), (c, 2), (x, 4), (y, 4)))

    def peer(g, j):
        dz, dc, dx, dy = offset_at(g, j)
        return zs[dz] * 2 + cs[dc], xs[dx] * 4 + ys[dy]

    lons = [peer(0, j)[1] for j in range(GRP)]

    def members(g):
        return GRP if g < N_GRP - 1 else GRP - 1

    def each_peer(fn):
        for g in range(N_GRP):
            for j in range(members(g)):
                fn(g, j, *peer(g, j))

    def remote(src, dst, send, recv, to_lat, to_lon):
        return pltpu.make_async_remote_copy(
            src_ref=src, dst_ref=dst, send_sem=send, recv_sem=recv,
            device_id=(to_lat, to_lon), device_id_type=MESH,
        )

    def wait_sent(ref, sem):
        remote(ref, ref, sem, sem, lat, lon).wait_send()

    def wait_got(ref, sem):
        remote(ref, ref, sem, sem, lat, lon).wait_recv()

    dep[...] = jnp.zeros_like(dep)
    recv_cot[0] = jnp.zeros(recv_cot.shape[1:], BF16)
    recv_cot[TLAT + 1] = jnp.zeros(recv_cot.shape[1:], BF16)

    barrier = pltpu.get_barrier_semaphore()

    def greet(g, j, to_lat, to_lon):
        pl.semaphore_signal(barrier, inc=1, device_id=(to_lat, to_lon), device_id_type=MESH)

    each_peer(greet)

    ins[0].wait()
    ins[1].wait()
    owner = owner_ref[...]
    valid = iota((1, OBS), 1) < count_ref[0]
    o_lat, o_lon = owner // GRP, owner % GRP
    dz, dc = (o_lat // 2 - z + 4) % 4, (o_lat - c + 2) % 2
    dx, dy = (o_lon // 4 - x + 4) % 4, (o_lon - y + 4) % 4
    group = (1 - dc) * 4 + (dz + dx + dy + 3) % 4
    rel = group * GRP + (dx + 3) % 4 * 4 + (dy + 3) % 4
    rel = jnp.where(valid, rel, -1)
    upto = jnp.where(iota((256, 256), 0) <= iota((256, 256), 1), 1.0, 0.0).astype(BF16)
    peer_ids = iota((N_DEV, 256), 0)
    carry = jnp.zeros((N_DEV, 1), F32)
    ranks = []
    for i in range(OBS // 256):
        hit = jnp.where(peer_ids == rel[:, i * 256 : (i + 1) * 256], 1.0, 0.0)
        count = mm(hit.astype(BF16), upto) + carry
        ranks.append(jnp.sum(hit * count, axis=0, keepdims=True) - 1.0)
        carry = count[:, 255:256]
    rank = jnp.concatenate(ranks, axis=1).astype(I32)
    key = jnp.where(valid, rel * CAP + rank, -1)

    value = cell_ref[...].reshape(1, OBS) + 1
    high = jnp.where(value >= 256, 1.0, 0.0)
    low = value.astype(F32) - 256.0 * high
    cells_high = jnp.zeros((N_DEV, 128), F32)
    cells_low = jnp.zeros((N_DEV, 128), F32)
    for i in range(OBS // 256):
        part = slice(i * 256, (i + 1) * 256)
        hit = jnp.where(peer_ids == rel[:, part], 1.0, 0.0)
        place = jnp.where(iota((128, 256), 0) == rank[:, part], 1.0, 0.0).astype(BF16)
        cells_high += mm_nt((hit * high[:, part]).astype(BF16), place)
        cells_low += mm_nt((hit * low[:, part]).astype(BF16), place)
    cells = (256.0 * cells_high + cells_low).reshape(N_GRP, GRP, 128)
    send_cells[...] = cells
    recv_cells[N_GRP - 1, GRP - 1 :] = cells[N_GRP - 1, GRP - 1 :]

    ins[2].wait()
    where_from = iota((GRP * 32, GLON), 0)
    tile, slot = where_from // 32, where_from % 32
    column = jnp.where(
        slot < TLON,
        tile * TLON + slot,
        jnp.where(
            slot == TLON,
            (tile * TLON + GLON - 1) % GLON,
            jnp.where(slot == TLON + 1, (tile * TLON + TLON) % GLON, -1),
        ),
    )
    pick = jnp.where(column == iota((GRP * 32, GLON), 1), 1.0, 0.0).astype(BF16)
    send_cot[...] = mm(pick, cot_ref[...]).reshape(GRP, 32, CH).astype(BF16)
    recv_cot[1 + lon] = send_cot[lon]

    ins[3].wait()

    def pack(g):
        total = jnp.zeros((SLOTS, FEAT), F32)
        for i in range(OBS // 256):
            part = slice(i * 256, (i + 1) * 256)
            take = jnp.where(iota((SLOTS, 256), 0) + g * SLOTS == key[:, part], 1.0, 0.0)
            total += mm(take.astype(BF16), obs_ref[part, :])
        send_rows[g * GRP : (g + 1) * GRP] = total.reshape(GRP, CAP, FEAT).astype(BF16)

    def send_group(g):
        for j in range(members(g)):
            remote(
                send_rows.at[g * GRP + j], recv_rows.at[g * GRP + j],
                row_send.at[g], row_recv.at[g], *peer(g, j),
            ).start()

    for g in range(EARLY):
        pack(g)

    pl.semaphore_wait(barrier, N_DEV - 1)

    def send_cell(g, j, to_lat, to_lon):
        remote(
            send_cells.at[g, pl.ds(j, 1)], recv_cells.at[g, pl.ds(j, 1)],
            cell_send.at[g], cell_recv.at[g], to_lat, to_lon,
        ).start()

    each_peer(send_cell)
    for j in range(GRP - 1):
        remote(
            send_cot.at[lons[j]], recv_cot.at[1 + lon], cot_send, cot_recv, lat, lons[j]
        ).start()

    @pl.when(up_edge)
    def _():
        for j in range(GRP):
            remote(
                send_cot.at[lons[j]], recv_cot.at[TLAT + 1], edge_send.at[0], edge_recv.at[0],
                lat - 1, lons[j],
            ).start()

    @pl.when(down_edge)
    def _():
        for j in range(GRP):
            remote(
                send_cot.at[lons[j]], recv_cot.at[0], edge_send.at[1], edge_recv.at[1],
                lat + 1, lons[j],
            ).start()

    for g in range(EARLY):
        send_group(g)

    for g in range(EARLY, N_GRP):
        pack(g)
        send_group(g)
    recv_rows[N_DEV - 1] = send_rows[N_DEV - 1]

    for copy in ins[4:]:
        copy.wait()
    w_in_t = w_in_ref[...].astype(F32).T.astype(BF16)
    w_out = w_out_ref[...]
    w_out_t = w_out.astype(F32).T.astype(BF16)
    bias_t = jnp.broadcast_to(bias_ref[...], (128, HID)).T[:, 0:1]
    for g in range(N_GRP):
        wait_got(recv_cells.at[g, pl.ds(0, members(g))], cell_recv.at[g])
    codes = recv_cells[...].reshape(N_DEV, 128)
    high = jnp.where(codes >= 256.0, 1.0, 0.0)
    spread = jnp.where(iota((128, SLOTS), 0) == iota((128, SLOTS), 1) % CAP, 1.0, 0.0).astype(BF16)
    codes = 256.0 * mm(high.astype(BF16), spread) + mm((codes - 256.0 * high).astype(BF16), spread)
    own = iota((GRP, SLOTS), 0) == iota((GRP, SLOTS), 1) // CAP
    for g in range(N_GRP):
        mine = jnp.where(own, codes[g * GRP : (g + 1) * GRP], 0.0)
        cell_of = jnp.sum(mine, axis=0, keepdims=True).astype(I32) - 1
        hit = jnp.where(iota((CELLS, SLOTS), 0) == cell_of, 1.0, 0.0)
        at = g % STEP * SLOTS
        places[g // STEP, :, at : at + SLOTS] = hit.astype(BF16)

    wait_got(recv_cot.at[pl.ds(0, GRP - 1)], cot_recv)

    @pl.when(lat < N_GRP - 1)
    def _():
        wait_got(recv_cot.at[TLAT + 1], edge_recv.at[0])

    @pl.when(lat > 0)
    def _():
        wait_got(recv_cot.at[0], edge_recv.at[1])

    cot_all = recv_cot[...].astype(F32)
    cot_f[:, 8:32, :] = cot_all[:, 0:TLON]
    cot_f[:, 7:8, :] = cot_all[:, TLON : TLON + 1]
    cot_f[:, 32:33, :] = cot_all[:, TLON + 1 : TLON + 2]

    for b in (-1, 0, 1):
        cot_s[b + 1] = cot_f[:, 8 - b : 8 - b + TLON, :]

    def adjoint_row(r, carry):
        total = jnp.zeros((TLON, CH), F32)
        for k, (a, b) in enumerate(TAPS):
            total += taps_ref[k : k + 1, :] * cot_s[b + 1, r + 1 - a]
        send_grid[r] = (SCALE * total).astype(BF16)
        return carry

    lax.fori_loop(0, TLAT, adjoint_row, 0)
    adj_t[...] = send_grid[...].astype(F32).reshape(CELLS, CH).T.astype(BF16)

    for i in range(N_STEP):
        up = mm(adj_t[...], places[i]).astype(BF16)
        ups[i] = up
        backs[i] = mm(w_out, up)

    acc_in[...] = jnp.zeros_like(acc_in)
    acc_out[...] = jnp.zeros_like(acc_out)
    acc_bias[...] = jnp.zeros_like(acc_bias)

    def work(i):
        rows = recv_rows[i * STEP * GRP : (i + 1) * STEP * GRP]
        rows = rows.astype(F32).reshape(WIDE, FEAT).astype(BF16)
        before = mm_nt(w_in_t, rows) + bias_t
        square = before * before
        t = jnp.tanh(C0 * before * (1.0 + C1 * square))
        half = 0.5 * (1.0 + t)
        slope = half + 0.5 * before * (1.0 - t * t) * (C0 * (1.0 + 3.0 * C1 * square))
        hidden = (before * half).astype(BF16)
        pre = (backs[i] * slope).astype(BF16)
        encoded = mm(w_out_t, hidden).astype(BF16)
        add = mm_nt(places[i], encoded).reshape(TLAT, TLON, CH)
        dep[1 : 1 + TLAT, 8 : 8 + TLON, :] += add
        acc_out[...] += mm_nt(hidden, ups[i])
        acc_in[...] += mm(pre, rows)
        pre = pre.astype(F32)
        acc_bias[...] += sum(pre[:, k * 128 : (k + 1) * 128] for k in range(WIDE // 128))

    for i in range(N_STEP):
        for g in range(i * STEP, (i + 1) * STEP):
            wait_got(recv_rows.at[pl.ds(g * GRP, members(g))], row_recv.at[g])
        work(i)

    north, south = lat > 0, lat < N_GRP - 1
    west, east = lax.rem(lon + 15, GRP), lax.rem(lon + 1, GRP)
    core = (1, TLAT)
    first, last = (1, 1), (TLAT, 1)
    above, below = (0, 1), (TLAT + 1, 1)
    wide, left, right = (8, TLON), (8, 1), (8 + TLON - 1, 1)
    before_left, after_right = (7, 1), (8 + TLON, 1)
    halos = [
        (None, lat, west, core, left, core, after_right),
        (None, lat, east, core, right, core, before_left),
        (north, lat - 1, lon, first, wide, below, wide),
        (south, lat + 1, lon, last, wide, above, wide),
        (north, lat - 1, west, first, left, below, after_right),
        (north, lat - 1, east, first, right, below, before_left),
        (south, lat + 1, west, last, left, above, after_right),
        (south, lat + 1, east, last, right, above, before_left),
    ]
    comes = [None, None, south, north, south, south, north, north]

    def at(rows, columns):
        return dep.at[pl.ds(*rows), pl.ds(*columns), :]

    for i, (there, to_lat, to_lon, sr, sc, dr, dc) in enumerate(halos):
        def send_halo(i=i, to_lat=to_lat, to_lon=to_lon, sr=sr, sc=sc, dr=dr, dc=dc):
            remote(
                at(sr, sc), at(dr, dc), halo_send.at[i], halo_recv.at[i], to_lat, to_lon
            ).start()

        send_halo() if there is None else pl.when(there)(send_halo)

    def taps_row(r, totals):
        for at in range(0, TLON, 8):
            mine = dep[r + 1, 8 + at : 16 + at, :]
            totals = tuple(
                total + mine * cot_s[b + 1, r + 1 - a, at : at + 8]
                for total, (a, b) in zip(totals, TAPS)
            )
        return totals

    totals = lax.fori_loop(0, TLAT, taps_row, (jnp.zeros((8, CH), F32),) * 9)
    small = [SCALE * jnp.sum(t, axis=0, keepdims=True) for t in totals]
    small.append(jnp.sum(acc_bias[...].T, axis=0, keepdims=True))
    small = [h for s in small for h in (s[:, :128], s[:, 128:])]
    small = jnp.concatenate(small + [jnp.zeros((4, 128), F32)], axis=0)
    small_high = small.astype(BF16)
    small_low = (small - small_high.astype(F32)).astype(BF16)
    chunks[0:32] = acc_in[...].reshape(32, 8, 128).astype(BF16)
    chunks[32:64] = acc_out[:, :128].reshape(32, 8, 128).astype(BF16)
    chunks[64:96] = acc_out[:, 128:].reshape(32, 8, 128).astype(BF16)
    chunks[96:99] = small_high.astype(F32).reshape(3, 8, 128).astype(BF16)
    chunks[99:102] = small_low.astype(F32).reshape(3, 8, 128).astype(BF16)
    chunks[102:128] = jnp.zeros((26, 8, 128), BF16)

    def send_part(g, j, to_lat, to_lon):
        remote(
            chunks.at[to_lat * GRP + to_lon], parts.at[g * GRP + j],
            part_send.at[g], part_recv.at[g], to_lat, to_lon,
        ).start()

    each_peer(send_part)
    parts[N_DEV - 1] = chunks[me]

    for i, there in enumerate(comes):
        _, _, _, _, _, dr, dc = halos[i]
        def got_halo(i=i, dr=dr, dc=dc):
            wait_got(at(dr, dc), halo_recv.at[i])

        got_halo() if there is None else pl.when(there)(got_halo)

    def grid_row(r, carry):
        total = jnp.zeros((TLON, CH), F32)
        for k, (a, b) in enumerate(TAPS):
            total += taps_ref[k : k + 1, :] * dep[r + 1 + a, 8 + b : 8 + b + TLON, :]
        send_grid[r] = total.astype(BF16)
        return carry

    lax.fori_loop(0, TLAT, grid_row, 0)
    for j in range(GRP - 1):
        remote(
            send_grid.at[lons[j]], grid_ref.at[lon], grid_send, grid_recv, lat, lons[j]
        ).start()
    mine_grid = pltpu.make_async_copy(send_grid.at[lon], grid_ref.at[lon], own_sem.at[0])
    mine_grid.start()

    for g in range(N_GRP):
        wait_got(parts.at[pl.ds(g * GRP, members(g))], part_recv.at[g])
    mine = jnp.sum(parts[...].astype(F32), axis=0).astype(BF16)
    red[...] = mine
    mine_share = pltpu.make_async_copy(red, shared.at[me], own_sem.at[1])
    mine_share.start()

    def send_share(g, j, to_lat, to_lon):
        remote(
            red, shared.at[me], share_send.at[g], share_recv.at[g], to_lat, to_lon
        ).start()

    each_peer(send_share)

    for g in range(N_GRP):
        wait_got(shared.at[pl.ds(g * GRP, members(g))], share_recv.at[g])
    mine_grid.wait()
    mine_share.wait()
    wait_got(grid_ref.at[pl.ds(0, GRP - 1)], grid_recv)
    for g in range(N_GRP):
        n = members(g)
        wait_sent(send_cells.at[g, pl.ds(0, n)], cell_send.at[g])
        wait_sent(send_rows.at[pl.ds(g * GRP, n)], row_send.at[g])
        wait_sent(chunks.at[pl.ds(g * GRP, n)], part_send.at[g])
        wait_sent(shared.at[pl.ds(g * GRP, n)], share_send.at[g])
    wait_sent(send_cot.at[pl.ds(0, GRP - 1)], cot_send)
    wait_sent(send_grid.at[pl.ds(0, GRP - 1)], grid_send)

    @pl.when(up_edge)
    def _():
        wait_sent(send_cot, edge_send.at[0])

    @pl.when(down_edge)
    def _():
        wait_sent(send_cot, edge_send.at[1])

    for i, (there, _, _, sr, sc, _, _) in enumerate(halos):
        def sent_halo(i=i, sr=sr, sc=sc):
            wait_sent(at(sr, sc), halo_send.at[i])

        sent_halo() if there is None else pl.when(there)(sent_halo)


def finish(
    grid_in, shared_in, grid_hbm, g_in_hbm, g_bias_hbm, g_out_hbm, g_taps_hbm,
    grid, shared, g_in, g_bias, g_out, g_taps, sem,
):
    come = pltpu.make_async_copy(shared_in, shared, sem.at[5])
    come.start()
    grid_come = pltpu.make_async_copy(grid_in, grid, sem.at[6])
    grid_come.start()
    copies = [pltpu.make_async_copy(grid, grid_hbm, sem.at[0])]
    come.wait()
    g_out[:, :128] = shared[32:64].astype(F32).reshape(HID, 128)
    g_out[:, 128:] = shared[64:96].astype(F32).reshape(HID, 128)
    copies.append(pltpu.make_async_copy(g_out, g_out_hbm, sem.at[1]))
    copies[1].start()
    g_in[...] = shared[0:32].astype(F32).reshape(HID, FEAT).T
    copies.append(pltpu.make_async_copy(g_in, g_in_hbm, sem.at[2]))
    copies[2].start()
    grid_come.wait()
    copies[0].start()
    small = (shared[96:99].astype(F32) + shared[99:102].astype(F32)).reshape(24, 128)
    for k in range(9):
        g_taps[k : k + 1, :128] = small[2 * k : 2 * k + 1]
        g_taps[k : k + 1, 128:] = small[2 * k + 1 : 2 * k + 2]
    g_bias[:, :128] = small[18:19]
    g_bias[:, 128:] = small[19:20]
    copies.append(pltpu.make_async_copy(g_taps, g_taps_hbm, sem.at[3]))
    copies.append(pltpu.make_async_copy(g_bias, g_bias_hbm, sem.at[4]))
    copies[3].start()
    copies[4].start()
    for copy in copies:
        copy.wait()


def local(obs, owner, cell, count, w_in, bias, w_out, taps, cot):
    smem = pl.BlockSpec(memory_space=pltpu.SMEM)
    hbm = pl.BlockSpec(memory_space=pltpu.HBM)
    dma = pltpu.SemaphoreType.DMA
    rows, shared = pl.pallas_call(
        kernel,
        name="encode_step",
        out_shape=(
            jax.ShapeDtypeStruct((GRP, TLON, CH), BF16),
            jax.ShapeDtypeStruct((N_DEV, 8, 128), BF16),
        ),
        in_specs=[hbm, hbm, hbm, smem, hbm, hbm, hbm, hbm, hbm],
        out_specs=(hbm,) * 2,
        scratch_shapes=[
            pltpu.VMEM((OBS, FEAT), BF16),
            pltpu.VMEM((1, OBS), I32),
            pltpu.VMEM((OBS,), I32),
            pltpu.VMEM((FEAT, HID), BF16),
            pltpu.VMEM((1, HID), F32),
            pltpu.VMEM((HID, CH), BF16),
            pltpu.VMEM((9, CH), F32),
            pltpu.VMEM((GLON, CH), BF16),
            pltpu.VMEM((N_DEV, CAP, FEAT), BF16),
            pltpu.VMEM((N_DEV, CAP, FEAT), BF16),
            pltpu.VMEM((N_GRP, GRP, 128), F32),
            pltpu.VMEM((N_GRP, GRP, 128), F32),
            pltpu.VMEM((GRP, 32, CH), BF16),
            pltpu.VMEM((TLAT + 2, 32, CH), BF16),
            pltpu.VMEM((TLAT + 2, 40, CH), F32),
            pltpu.VMEM((3, TLAT + 2, TLON, CH), F32),
            pltpu.VMEM((TLAT + 2, 40, CH), F32),
            pltpu.VMEM((TLAT, TLON, CH), BF16),
            pltpu.VMEM((N_DEV, 8, 128), BF16),
            pltpu.VMEM((N_DEV, 8, 128), BF16),
            pltpu.VMEM((8, 128), BF16),
            pltpu.VMEM((HID, FEAT), F32),
            pltpu.VMEM((HID, CH), F32),
            pltpu.VMEM((HID, 128), F32),
            pltpu.VMEM((CH, CELLS), BF16),
            pltpu.VMEM((N_STEP, CELLS, WIDE), BF16),
            pltpu.VMEM((N_STEP, HID, WIDE), BF16),
            pltpu.VMEM((N_STEP, HID, WIDE), F32),
            dma((8,)), dma((2,)),
            dma((N_GRP,)), dma((N_GRP,)), dma((N_GRP,)), dma((N_GRP,)),
            dma, dma, dma((2,)), dma((2,)),
            dma((N_GRP,)), dma((N_GRP,)), dma((N_GRP,)), dma((N_GRP,)),
            dma((8,)), dma((8,)), dma, dma,
        ],
        compiler_params=pltpu.CompilerParams(
            collective_id=0, has_side_effects=True, vmem_limit_bytes=67043328
        ),
        cost_estimate=pl.CostEstimate(
            flops=4_000_000_000, bytes_accessed=2_000_000, transcendentals=800_000
        ),
    )(
        obs, owner.reshape(1, OBS), cell, count, w_in, bias.reshape(1, HID),
        w_out, taps, cot.reshape(GLON, CH),
    )
    outs = [((GRP, TLON, CH), BF16), ((FEAT, HID), F32), ((1, HID), F32), ((HID, CH), F32), ((9, CH), F32)]
    grid, g_in, g_bias, g_out, g_taps = pl.pallas_call(
        finish,
        name="finish",
        out_shape=tuple(jax.ShapeDtypeStruct(*o) for o in outs),
        in_specs=[hbm, hbm],
        out_specs=(hbm,) * 5,
        scratch_shapes=[
            pltpu.VMEM(*outs[0]),
            pltpu.VMEM((N_DEV, 8, 128), BF16),
            *[pltpu.VMEM(*o) for o in outs[1:]],
            dma((7,)),
        ],
        compiler_params=pltpu.CompilerParams(vmem_limit_bytes=67043328),
    )(rows, shared)
    return (grid.reshape(1, GLON, CH), g_in, g_bias.reshape(HID), g_out, g_taps)


def solution(mesh):
    block = P(("lat", "lon"))
    return jax.shard_map(
        local,
        mesh=mesh,
        in_specs=(block, block, block, block, P(), P(), P(), P(), block),
        out_specs=(block, P(), P(), P(), P()),
        check_vma=False,
    )
```

time: 64.9 us -> 48.8 us (0.75)
  local copies, waits for them, and re-layouts: 8.27 us -> 0 us
  Pallas kernels: 54.9 us -> 47.1 us
    pallas_call x1, Pallas kernels: 54.9 us -> 45.3 us  [local(): pl.pallas_call(kernel, name='encode_step', out_shape=(jax.ShapeDtypeStruc...]
    unnamed x19 -> x0, local copies, waits for them, and re-layouts: 7.56 us -> none
    pallas_call x0 -> x1, Pallas kernels: none -> 1.86 us  [local(): pl.pallas_call(finish, name='finish', out_shape=tuple((jax.ShapeDtypeStru...]
    reshape x1 -> x0, local copies, waits for them, and re-layouts: 0.71 us -> none  [local(): cell.reshape(1, OBS)]
where the time goes in v2:
time: 48.8 us; the launch traced here: 48.6 us
  Pallas kernels  47.1 us (97%)
  between operations  1.45 us (3%)
    pallas_call x1, Pallas kernels, local(): pl.pallas_call(kernel, name='encode_step', out_shape=(jax.ShapeDtypeStruc...  45.3 us
    pallas_call x1, Pallas kernels, local(): pl.pallas_call(finish, name='finish', out_shape=tuple((jax.ShapeDtypeStru...  1.86 us

profile of v2, /device:TPU:1, one launch (start us, length us, event | category | flops | bytes accessed | tf_op | source)
XLA Modules:
  0.0 48.6 jit_solution(7968255431782664062)
XLA Ops:
  1.3 45.3 %encode_step.1 = (bf16[16,24,256]{2,1,0:T(8,128)(2,1)}, bf16[128,8,128]{2,1,0:T(8,128)(2,1)}) custom-call(bf16[1536,128]{1,0:T(8,128)(2,1)} %obs_hbm.1, s32[1,1536]{1,0:T(1,128)} %bitcast.7, s32[1536]{0:T(1024)} %cell_hbm.1, s32[1]{0:T(128)S(6)} %copy.14.count_ref, bf16[128,256]{1,0:T(8,128)(2,1)} %w_in_hbm.1, f32[1,256]{1,0:T(1,128)} %bitcast.8, ...), custom_call_target="tpu_custom_call" | custom-call | flops 4000000000 | bytes 2000000 | tf_op jit(solution)/shard_map/encode_step/pallas_call | solution.py:468
  46.6 1.9 %finish.1 = (bf16[16,24,256]{2,1,0:T(8,128)(2,1)}, f32[128,256]{1,0:T(8,128)}, f32[1,256]{1,0:T(1,128)}, f32[256,256]{1,0:T(8,128)}, f32[9,256]{1,0:T(8,128)}) custom-call(bf16[16,24,256]{2,1,0:T(8,128)(2,1)} %get-tuple-element.12.grid_in, bf16[128,8,128]{2,1,0:T(8,128)(2,1)} %get-tuple-element.13.shared_in), custom_call_target="tpu_custom_call" | custom-call | tf_op jit(solution)/shard_map/finish/pallas_call | solution.py:523

commit v3 on v2

--- a/solution.py
+++ b/solution.py
@@ -3,6 +3,7 @@
 
 import jax
 import jax.numpy as jnp
+import numpy as np
 from jax import lax
 from jax.experimental import pallas as pl
 from jax.experimental.pallas import tpu as pltpu
@@ -14,15 +15,14 @@
 TAPS = [(a, b) for a in (-1, 0, 1) for b in (-1, 0, 1)]
 
 N_DEV, N_GRP, GRP = 128, 8, 16
-EARLY = 4
-STEP = 2
-N_STEP = N_GRP // STEP
+EARLY = 3
+HOLD = 7
+STEPS = ((0, 1), (2, 3), (4, 5), (6, 7))
 OBS, FEAT, HID, CH = 1536, 128, 256, 256
 CAP = 24
 SLOTS = GRP * CAP
 TLAT, TLON = 16, 24
 CELLS = TLAT * TLON
-WIDE = STEP * SLOTS
 GLON = 384
 CHUNKS_IN, CHUNKS_OUT, CHUNKS_SMALL = 32, 64, 3
 SCALE = 1.0 / math.sqrt(OBS * N_DEV)
@@ -41,17 +41,22 @@
     return lax.dot_general(a, b, NT, preferred_element_type=F32)
 
 
-def offset_at(g, j):
-    dx, dy = (j // 4 + 1) % 4, (j + 1) % 4
-    return (g + 1 - dx - dy) % 4, (g // 4 + 1) % 2, dx, dy
+def hops(offset):
+    dz, dc, dx, dy = offset
+    return sum(min(d, 4 - d) for d in (dz, dx, dy)) + 0.1 * dc
+
+
+PLACES = sorted(
+    ((i // 32, i // 16 % 2, i // 4 % 4, i % 4) for i in range(N_DEV)), key=hops, reverse=True
+)
 
 
 def kernel(
-    obs_hbm, owner_hbm, cell_hbm, count_ref, w_in_hbm, bias_hbm, w_out_hbm, taps_hbm, cot_hbm,
+    obs_hbm, owner_hbm, cell_hbm, count_hbm, order_hbm, w_in_hbm, bias_hbm, w_out_hbm, taps_hbm, cot_hbm,
     grid_ref, shared,
-    obs_ref, owner_ref, cell_ref, w_in_ref, bias_ref, w_out_ref, taps_ref, cot_ref,
+    obs_ref, owner_ref, cell_ref, count_ref, order_ref, w_in_ref, bias_ref, w_out_ref, taps_ref, cot_ref,
     send_rows, recv_rows, send_cells, recv_cells, send_cot, recv_cot, cot_f, cot_s, dep, send_grid,
-    chunks, parts, red, acc_in, acc_out, acc_bias, adj_t, places, ups, backs,
+    chunks, parts, red, acc_in, acc_out, adj_t, places, ups, backs,
     in_sem, own_sem,
     row_send, row_recv, cell_send, cell_recv, cot_send, cot_recv, edge_send, edge_recv,
     part_send, part_recv, share_send, share_recv, halo_send, halo_recv, grid_send, grid_recv,
@@ -59,7 +64,7 @@
     ins = [
         pltpu.make_async_copy(src, dst, in_sem.at[i])
         for i, (src, dst) in enumerate([
-            (owner_hbm, owner_ref), (cell_hbm, cell_ref), (cot_hbm, cot_ref), (obs_hbm, obs_ref),
+            (owner_hbm, owner_ref), (count_hbm, count_ref), (order_hbm, order_ref), (cell_hbm, cell_ref), (cot_hbm, cot_ref), (obs_hbm, obs_ref),
             (w_in_hbm, w_in_ref), (w_out_hbm, w_out_ref), (bias_hbm, bias_ref), (taps_hbm, taps_ref),
         ])
     ]
@@ -74,10 +79,11 @@
     zs, cs, xs, ys = ([lax.rem(at + d, n) for d in range(n)] for at, n in ((z, 4), (c, 2), (x, 4), (y, 4)))
 
     def peer(g, j):
-        dz, dc, dx, dy = offset_at(g, j)
+        dz, dc, dx, dy = PLACES[g * GRP + j]
         return zs[dz] * 2 + cs[dc], xs[dx] * 4 + ys[dy]
 
-    lons = [peer(0, j)[1] for j in range(GRP)]
+    plane = [d for d in PLACES if d[:2] == (0, 0)]
+    lons = [xs[dx] * 4 + ys[dy] for _, _, dx, dy in plane]
 
     def members(g):
         return GRP if g < N_GRP - 1 else GRP - 1
@@ -99,6 +105,7 @@
     def wait_got(ref, sem):
         remote(ref, ref, sem, sem, lat, lon).wait_recv()
 
+
     dep[...] = jnp.zeros_like(dep)
     recv_cot[0] = jnp.zeros(recv_cot.shape[1:], BF16)
     recv_cot[TLAT + 1] = jnp.zeros(recv_cot.shape[1:], BF16)
@@ -110,27 +117,31 @@
 
     each_peer(greet)
 
-    ins[0].wait()
-    ins[1].wait()
+
+    for copy in ins[:4]:
+        copy.wait()
     owner = owner_ref[...]
     valid = iota((1, OBS), 1) < count_ref[0]
     o_lat, o_lon = owner // GRP, owner % GRP
     dz, dc = (o_lat // 2 - z + 4) % 4, (o_lat - c + 2) % 2
     dx, dy = (o_lon // 4 - x + 4) % 4, (o_lon - y + 4) % 4
-    group = (1 - dc) * 4 + (dz + dx + dy + 3) % 4
-    rel = group * GRP + (dx + 3) % 4 * 4 + (dy + 3) % 4
+    rel = dz * 32 + dc * 16 + dx * 4 + dy
     rel = jnp.where(valid, rel, -1)
     upto = jnp.where(iota((256, 256), 0) <= iota((256, 256), 1), 1.0, 0.0).astype(BF16)
-    peer_ids = iota((N_DEV, 256), 0)
+    order = jnp.concatenate([order_ref[...]] * 2, axis=1)
+    base = (iota((N_DEV, 256), 0) * CAP).astype(F32)
     carry = jnp.zeros((N_DEV, 1), F32)
-    ranks = []
+    ranks, keys, hits = [], [], []
     for i in range(OBS // 256):
-        hit = jnp.where(peer_ids == rel[:, i * 256 : (i + 1) * 256], 1.0, 0.0)
+        hit = jnp.where(order == rel[:, i * 256 : (i + 1) * 256], 1.0, 0.0)
         count = mm(hit.astype(BF16), upto) + carry
         ranks.append(jnp.sum(hit * count, axis=0, keepdims=True) - 1.0)
+        keys.append(jnp.sum(hit * (count + base), axis=0, keepdims=True) - 1.0)
         carry = count[:, 255:256]
+        hits.append(hit)
     rank = jnp.concatenate(ranks, axis=1).astype(I32)
-    key = jnp.where(valid, rel * CAP + rank, -1)
+    key = jnp.concatenate(keys, axis=1).astype(I32)
+
 
     value = cell_ref[...].reshape(1, OBS) + 1
     high = jnp.where(value >= 256, 1.0, 0.0)
@@ -139,7 +150,7 @@
     cells_low = jnp.zeros((N_DEV, 128), F32)
     for i in range(OBS // 256):
         part = slice(i * 256, (i + 1) * 256)
-        hit = jnp.where(peer_ids == rel[:, part], 1.0, 0.0)
+        hit = hits[i]
         place = jnp.where(iota((128, 256), 0) == rank[:, part], 1.0, 0.0).astype(BF16)
         cells_high += mm_nt((hit * high[:, part]).astype(BF16), place)
         cells_low += mm_nt((hit * low[:, part]).astype(BF16), place)
@@ -147,7 +158,8 @@
     send_cells[...] = cells
     recv_cells[N_GRP - 1, GRP - 1 :] = cells[N_GRP - 1, GRP - 1 :]
 
-    ins[2].wait()
+
+    ins[4].wait()
     where_from = iota((GRP * 32, GLON), 0)
     tile, slot = where_from // 32, where_from % 32
     column = jnp.where(
@@ -160,10 +172,11 @@
         ),
     )
     pick = jnp.where(column == iota((GRP * 32, GLON), 1), 1.0, 0.0).astype(BF16)
-    send_cot[...] = mm(pick, cot_ref[...]).reshape(GRP, 32, CH).astype(BF16)
+    send_cot[...] = mm(pick, cot_ref[...]).reshape(GRP, 32, CH)[:, :26].astype(BF16)
     recv_cot[1 + lon] = send_cot[lon]
 
-    ins[3].wait()
+
+    ins[5].wait()
 
     def pack(g):
         total = jnp.zeros((SLOTS, FEAT), F32)
@@ -183,7 +196,9 @@
     for g in range(EARLY):
         pack(g)
 
+
     pl.semaphore_wait(barrier, N_DEV - 1)
+
 
     def send_cell(g, j, to_lat, to_lon):
         remote(
@@ -213,15 +228,18 @@
                 lat + 1, lons[j],
             ).start()
 
-    for g in range(EARLY):
+
+    for g in range(EARLY, HOLD):
+        pack(g)
+    for g in range(HOLD):
         send_group(g)
-
-    for g in range(EARLY, N_GRP):
+    for g in range(HOLD, N_GRP):
         pack(g)
         send_group(g)
     recv_rows[N_DEV - 1] = send_rows[N_DEV - 1]
 
-    for copy in ins[4:]:
+
+    for copy in ins[6:]:
         copy.wait()
     w_in_t = w_in_ref[...].astype(F32).T.astype(BF16)
     w_out = w_out_ref[...]
@@ -234,30 +252,24 @@
     spread = jnp.where(iota((128, SLOTS), 0) == iota((128, SLOTS), 1) % CAP, 1.0, 0.0).astype(BF16)
     codes = 256.0 * mm(high.astype(BF16), spread) + mm((codes - 256.0 * high).astype(BF16), spread)
     own = iota((GRP, SLOTS), 0) == iota((GRP, SLOTS), 1) // CAP
+
     for g in range(N_GRP):
         mine = jnp.where(own, codes[g * GRP : (g + 1) * GRP], 0.0)
         cell_of = jnp.sum(mine, axis=0, keepdims=True).astype(I32) - 1
         hit = jnp.where(iota((CELLS, SLOTS), 0) == cell_of, 1.0, 0.0)
-        at = g % STEP * SLOTS
-        places[g // STEP, :, at : at + SLOTS] = hit.astype(BF16)
+        places[:, g * SLOTS : (g + 1) * SLOTS] = hit.astype(BF16)
+
 
     wait_got(recv_cot.at[pl.ds(0, GRP - 1)], cot_recv)
 
-    @pl.when(lat < N_GRP - 1)
-    def _():
-        wait_got(recv_cot.at[TLAT + 1], edge_recv.at[0])
-
-    @pl.when(lat > 0)
-    def _():
-        wait_got(recv_cot.at[0], edge_recv.at[1])
-
-    cot_all = recv_cot[...].astype(F32)
-    cot_f[:, 8:32, :] = cot_all[:, 0:TLON]
-    cot_f[:, 7:8, :] = cot_all[:, TLON : TLON + 1]
-    cot_f[:, 32:33, :] = cot_all[:, TLON + 1 : TLON + 2]
-
-    for b in (-1, 0, 1):
-        cot_s[b + 1] = cot_f[:, 8 - b : 8 - b + TLON, :]
+
+    def spread_cot(rows):
+        part = recv_cot[rows].astype(F32)
+        cot_f[rows, 8:32, :] = part[:, 0:TLON]
+        cot_f[rows, 7:8, :] = part[:, TLON : TLON + 1]
+        cot_f[rows, 32:33, :] = part[:, TLON + 1 : TLON + 2]
+        for b in (-1, 0, 1):
+            cot_s[b + 1, rows] = cot_f[rows, 8 - b : 8 - b + TLON, :]
 
     def adjoint_row(r, carry):
         total = jnp.zeros((TLON, CH), F32)
@@ -266,40 +278,59 @@
         send_grid[r] = (SCALE * total).astype(BF16)
         return carry
 
-    lax.fori_loop(0, TLAT, adjoint_row, 0)
+    spread_cot(slice(1, TLAT + 1))
+    lax.fori_loop(1, TLAT - 1, adjoint_row, 0)
+
+
+    @pl.when(lat < N_GRP - 1)
+    def _():
+        wait_got(recv_cot.at[TLAT + 1], edge_recv.at[0])
+
+    @pl.when(lat > 0)
+    def _():
+        wait_got(recv_cot.at[0], edge_recv.at[1])
+
+
+    for row in (0, TLAT + 1):
+        spread_cot(slice(row, row + 1))
+    adjoint_row(0, 0)
+    adjoint_row(TLAT - 1, 0)
     adj_t[...] = send_grid[...].astype(F32).reshape(CELLS, CH).T.astype(BF16)
 
-    for i in range(N_STEP):
-        up = mm(adj_t[...], places[i]).astype(BF16)
-        ups[i] = up
-        backs[i] = mm(w_out, up)
+
+    for i in range(0, N_GRP, 2):
+        at = slice(i * SLOTS, (i + 2) * SLOTS)
+        up = mm(adj_t[...], places[:, at]).astype(BF16)
+        ups[:, at] = up
+        backs[:, at] = mm(w_out, up)
 
     acc_in[...] = jnp.zeros_like(acc_in)
     acc_out[...] = jnp.zeros_like(acc_out)
-    acc_bias[...] = jnp.zeros_like(acc_bias)
-
-    def work(i):
-        rows = recv_rows[i * STEP * GRP : (i + 1) * STEP * GRP]
-        rows = rows.astype(F32).reshape(WIDE, FEAT).astype(BF16)
+
+    def work(groups):
+        start, count = groups[0], len(groups)
+        at = slice(start * SLOTS, (start + count) * SLOTS)
+        rows = recv_rows[start * GRP : (start + count) * GRP]
+        rows = rows.astype(F32).reshape(count * SLOTS, FEAT).astype(BF16)
         before = mm_nt(w_in_t, rows) + bias_t
         square = before * before
-        t = jnp.tanh(C0 * before * (1.0 + C1 * square))
-        half = 0.5 * (1.0 + t)
-        slope = half + 0.5 * before * (1.0 - t * t) * (C0 * (1.0 + 3.0 * C1 * square))
-        hidden = (before * half).astype(BF16)
-        pre = (backs[i] * slope).astype(BF16)
+        half = 0.5 + 0.5 * jnp.tanh(before * (C0 + C0 * C1 * square))
+        value = before * half
+        hidden = value.astype(BF16)
+        slope = half + value * (1.0 - half) * (2.0 * C0 + 6.0 * C0 * C1 * square)
+        pre = (backs[:, at] * slope).astype(BF16)
         encoded = mm(w_out_t, hidden).astype(BF16)
-        add = mm_nt(places[i], encoded).reshape(TLAT, TLON, CH)
+        add = mm_nt(places[:, at], encoded).reshape(TLAT, TLON, CH)
         dep[1 : 1 + TLAT, 8 : 8 + TLON, :] += add
-        acc_out[...] += mm_nt(hidden, ups[i])
-        acc_in[...] += mm(pre, rows)
-        pre = pre.astype(F32)
-        acc_bias[...] += sum(pre[:, k * 128 : (k + 1) * 128] for k in range(WIDE // 128))
-
-    for i in range(N_STEP):
-        for g in range(i * STEP, (i + 1) * STEP):
+        acc_out[...] += mm_nt(hidden, ups[:, at])
+        ones = jnp.ones((count * SLOTS, 128), BF16)
+        acc_in[...] += mm(pre, jnp.concatenate([rows, ones], axis=1))
+
+    for groups in STEPS:
+        for g in groups:
             wait_got(recv_rows.at[pl.ds(g * GRP, members(g))], row_recv.at[g])
-        work(i)
+        work(groups)
+
 
     north, south = lat > 0, lat < N_GRP - 1
     west, east = lax.rem(lon + 15, GRP), lax.rem(lon + 1, GRP)
@@ -331,6 +362,7 @@
 
         send_halo() if there is None else pl.when(there)(send_halo)
 
+
     def taps_row(r, totals):
         for at in range(0, TLON, 8):
             mine = dep[r + 1, 8 + at : 16 + at, :]
@@ -342,12 +374,13 @@
 
     totals = lax.fori_loop(0, TLAT, taps_row, (jnp.zeros((8, CH), F32),) * 9)
     small = [SCALE * jnp.sum(t, axis=0, keepdims=True) for t in totals]
-    small.append(jnp.sum(acc_bias[...].T, axis=0, keepdims=True))
+    small.append(acc_in[:, FEAT:].T[0:1])
     small = [h for s in small for h in (s[:, :128], s[:, 128:])]
     small = jnp.concatenate(small + [jnp.zeros((4, 128), F32)], axis=0)
     small_high = small.astype(BF16)
     small_low = (small - small_high.astype(F32)).astype(BF16)
-    chunks[0:32] = acc_in[...].reshape(32, 8, 128).astype(BF16)
+
+    chunks[0:32] = acc_in[:, :FEAT].reshape(32, 8, 128).astype(BF16)
     chunks[32:64] = acc_out[:, :128].reshape(32, 8, 128).astype(BF16)
     chunks[64:96] = acc_out[:, 128:].reshape(32, 8, 128).astype(BF16)
     chunks[96:99] = small_high.astype(F32).reshape(3, 8, 128).astype(BF16)
@@ -360,8 +393,10 @@
             part_send.at[g], part_recv.at[g], to_lat, to_lon,
         ).start()
 
+
     each_peer(send_part)
     parts[N_DEV - 1] = chunks[me]
+
 
     for i, there in enumerate(comes):
         _, _, _, _, _, dr, dc = halos[i]
@@ -369,6 +404,7 @@
             wait_got(at(dr, dc), halo_recv.at[i])
 
         got_halo() if there is None else pl.when(there)(got_halo)
+
 
     def grid_row(r, carry):
         total = jnp.zeros((TLON, CH), F32)
@@ -385,8 +421,10 @@
     mine_grid = pltpu.make_async_copy(send_grid.at[lon], grid_ref.at[lon], own_sem.at[0])
     mine_grid.start()
 
+
     for g in range(N_GRP):
         wait_got(parts.at[pl.ds(g * GRP, members(g))], part_recv.at[g])
+
     mine = jnp.sum(parts[...].astype(F32), axis=0).astype(BF16)
     red[...] = mine
     mine_share = pltpu.make_async_copy(red, shared.at[me], own_sem.at[1])
@@ -397,10 +435,13 @@
             red, shared.at[me], share_send.at[g], share_recv.at[g], to_lat, to_lon
         ).start()
 
+
     each_peer(send_share)
+
 
     for g in range(N_GRP):
         wait_got(shared.at[pl.ds(g * GRP, members(g))], share_recv.at[g])
+
     mine_grid.wait()
     mine_share.wait()
     wait_got(grid_ref.at[pl.ds(0, GRP - 1)], grid_recv)
@@ -462,9 +503,10 @@
 
 
 def local(obs, owner, cell, count, w_in, bias, w_out, taps, cot):
-    smem = pl.BlockSpec(memory_space=pltpu.SMEM)
     hbm = pl.BlockSpec(memory_space=pltpu.HBM)
     dma = pltpu.SemaphoreType.DMA
+    order = [dz * 32 + dc * 16 + dx * 4 + dy for dz, dc, dx, dy in PLACES]
+    order = jnp.asarray(np.repeat(np.array(order, np.int32)[:, None], 128, axis=1))
     rows, shared = pl.pallas_call(
         kernel,
         name="encode_step",
@@ -472,12 +514,14 @@
             jax.ShapeDtypeStruct((GRP, TLON, CH), BF16),
             jax.ShapeDtypeStruct((N_DEV, 8, 128), BF16),
         ),
-        in_specs=[hbm, hbm, hbm, smem, hbm, hbm, hbm, hbm, hbm],
+        in_specs=[hbm] * 10,
         out_specs=(hbm,) * 2,
         scratch_shapes=[
             pltpu.VMEM((OBS, FEAT), BF16),
             pltpu.VMEM((1, OBS), I32),
             pltpu.VMEM((OBS,), I32),
+            pltpu.SMEM((1,), I32),
+            pltpu.VMEM((N_DEV, 128), I32),
             pltpu.VMEM((FEAT, HID), BF16),
             pltpu.VMEM((1, HID), F32),
             pltpu.VMEM((HID, CH), BF16),
@@ -487,8 +531,8 @@
             pltpu.VMEM((N_DEV, CAP, FEAT), BF16),
             pltpu.VMEM((N_GRP, GRP, 128), F32),
             pltpu.VMEM((N_GRP, GRP, 128), F32),
-            pltpu.VMEM((GRP, 32, CH), BF16),
-            pltpu.VMEM((TLAT + 2, 32, CH), BF16),
+            pltpu.VMEM((GRP, 26, CH), BF16),
+            pltpu.VMEM((TLAT + 2, 26, CH), BF16),
             pltpu.VMEM((TLAT + 2, 40, CH), F32),
             pltpu.VMEM((3, TLAT + 2, TLON, CH), F32),
             pltpu.VMEM((TLAT + 2, 40, CH), F32),
@@ -496,14 +540,13 @@
             pltpu.VMEM((N_DEV, 8, 128), BF16),
             pltpu.VMEM((N_DEV, 8, 128), BF16),
             pltpu.VMEM((8, 128), BF16),
-            pltpu.VMEM((HID, FEAT), F32),
+            pltpu.VMEM((HID, 2 * FEAT), F32),
             pltpu.VMEM((HID, CH), F32),
-            pltpu.VMEM((HID, 128), F32),
             pltpu.VMEM((CH, CELLS), BF16),
-            pltpu.VMEM((N_STEP, CELLS, WIDE), BF16),
-            pltpu.VMEM((N_STEP, HID, WIDE), BF16),
-            pltpu.VMEM((N_STEP, HID, WIDE), F32),
-            dma((8,)), dma((2,)),
+            pltpu.VMEM((CELLS, N_GRP * SLOTS), BF16),
+            pltpu.VMEM((CH, N_GRP * SLOTS), BF16),
+            pltpu.VMEM((HID, N_GRP * SLOTS), F32),
+            dma((10,)), dma((2,)),
             dma((N_GRP,)), dma((N_GRP,)), dma((N_GRP,)), dma((N_GRP,)),
             dma, dma, dma((2,)), dma((2,)),
             dma((N_GRP,)), dma((N_GRP,)), dma((N_GRP,)), dma((N_GRP,)),
@@ -516,7 +559,7 @@
             flops=4_000_000_000, bytes_accessed=2_000_000, transcendentals=800_000
         ),
     )(
-        obs, owner.reshape(1, OBS), cell, count, w_in, bias.reshape(1, HID),
+        obs, owner.reshape(1, OBS), cell, count, order, w_in, bias.reshape(1, HID),
         w_out, taps, cot.reshape(GLON, CH),
     )
     outs = [((GRP, TLON, CH), BF16), ((FEAT, HID), F32), ((1, HID), F32), ((HID, CH), F32), ((9, CH), F32)]

time: 48.8 us -> 47.9 us (0.982)
  Pallas kernels: 47.1 us -> 46.3 us
    pallas_call x1, Pallas kernels: 45.3 us -> 44.4 us  [local(): pl.pallas_call(kernel, name='encode_step', out_shape=(jax.ShapeDtypeStruc...]
where the time goes in v3:
time: 47.9 us; the launch traced here: 47.7 us
  Pallas kernels  46.3 us (97%)
  between operations  1.45 us (3%)
    pallas_call x1, Pallas kernels, local(): pl.pallas_call(kernel, name='encode_step', out_shape=(jax.ShapeDtypeStruc...  44.4 us
    pallas_call x1, Pallas kernels, local(): pl.pallas_call(finish, name='finish', out_shape=tuple((jax.ShapeDtypeStru...  1.86 us

profile of v3, /device:TPU:1, one launch (start us, length us, event | category | flops | bytes accessed | tf_op | source)
XLA Modules:
  0.0 47.7 jit_solution(16173125265692067578)
XLA Ops:
  1.3 44.4 %encode_step.1 = (bf16[16,24,256]{2,1,0:T(8,128)(2,1)}, bf16[128,8,128]{2,1,0:T(8,128)(2,1)}) custom-call(bf16[1536,128]{1,0:T(8,128)(2,1)} %obs_hbm.1, s32[1,1536]{1,0:T(1,128)} %bitcast.7, s32[1536]{0:T(1024)} %cell_hbm.1, s32[1]{0:T(128)S(6)} %copy.15.count_hbm, s32[128,128]{1,0:T(8,128)} %constant.2.clone.order_hbm, bf16[128,256]{1,0:T(8,128)(2,1)} %w_in_hbm.1, ...), custom_call_target="tpu_custom_call" | custom-call | flops 4000000000 | bytes 2000000 | tf_op jit(solution)/shard_map/encode_step/pallas_call | solution.py:510
  45.7 1.9 %finish.1 = (bf16[16,24,256]{2,1,0:T(8,128)(2,1)}, f32[128,256]{1,0:T(8,128)}, f32[1,256]{1,0:T(1,128)}, f32[256,256]{1,0:T(8,128)}, f32[9,256]{1,0:T(8,128)}) custom-call(bf16[16,24,256]{2,1,0:T(8,128)(2,1)} %get-tuple-element.12.grid_in, bf16[128,8,128]{2,1,0:T(8,128)(2,1)} %get-tuple-element.13.shared_in), custom_call_target="tpu_custom_call" | custom-call | tf_op jit(solution)/shard_map/finish/pallas_call | solution.py:566

commit v4 on v3

--- a/solution.py
+++ b/solution.py
@@ -17,7 +17,7 @@
 N_DEV, N_GRP, GRP = 128, 8, 16
 EARLY = 3
 HOLD = 7
-STEPS = ((0, 1), (2, 3), (4, 5), (6, 7))
+STEPS = ((0, 1), (2, 3), (4, 5, 6, 7))
 OBS, FEAT, HID, CH = 1536, 128, 256, 256
 CAP = 24
 SLOTS = GRP * CAP
@@ -298,8 +298,8 @@
     adj_t[...] = send_grid[...].astype(F32).reshape(CELLS, CH).T.astype(BF16)
 
 
-    for i in range(0, N_GRP, 2):
-        at = slice(i * SLOTS, (i + 2) * SLOTS)
+    for i in range(0, N_GRP, 4):
+        at = slice(i * SLOTS, (i + 4) * SLOTS)
         up = mm(adj_t[...], places[:, at]).astype(BF16)
         ups[:, at] = up
         backs[:, at] = mm(w_out, up)
@@ -327,8 +327,10 @@
         acc_in[...] += mm(pre, jnp.concatenate([rows, ones], axis=1))
 
     for groups in STEPS:
+
         for g in groups:
             wait_got(recv_rows.at[pl.ds(g * GRP, members(g))], row_recv.at[g])
+
         work(groups)
 
 

time: 47.9 us -> 47.7 us (level)
  no operation moved by 1% of the time
where the time goes in v4:
time: 47.7 us; the launch traced here: 47.5 us
  Pallas kernels  46.1 us (97%)
  between operations  1.45 us (3%)
    pallas_call x1, Pallas kernels, local(): pl.pallas_call(kernel, name='encode_step', out_shape=(jax.ShapeDtypeStruc...  44.2 us
    pallas_call x1, Pallas kernels, local(): pl.pallas_call(finish, name='finish', out_shape=tuple((jax.ShapeDtypeStru...  1.86 us

profile of v4, /device:TPU:1, one launch (start us, length us, event | category | flops | bytes accessed | tf_op | source)
XLA Modules:
  0.0 47.5 jit_solution(9844738911649370275)
XLA Ops:
  1.3 44.2 %encode_step.1 = (bf16[16,24,256]{2,1,0:T(8,128)(2,1)}, bf16[128,8,128]{2,1,0:T(8,128)(2,1)}) custom-call(bf16[1536,128]{1,0:T(8,128)(2,1)} %obs_hbm.1, s32[1,1536]{1,0:T(1,128)} %bitcast.7, s32[1536]{0:T(1024)} %cell_hbm.1, s32[1]{0:T(128)S(6)} %copy.15.count_hbm, s32[128,128]{1,0:T(8,128)} %constant.2.clone.order_hbm, bf16[128,256]{1,0:T(8,128)(2,1)} %w_in_hbm.1, ...), custom_call_target="tpu_custom_call" | custom-call | flops 4000000000 | bytes 2000000 | tf_op jit(solution)/shard_map/encode_step/pallas_call | solution.py:512
  45.5 1.9 %finish.1 = (bf16[16,24,256]{2,1,0:T(8,128)(2,1)}, f32[128,256]{1,0:T(8,128)}, f32[1,256]{1,0:T(1,128)}, f32[256,256]{1,0:T(8,128)}, f32[9,256]{1,0:T(8,128)}) custom-call(bf16[16,24,256]{2,1,0:T(8,128)(2,1)} %get-tuple-element.12.grid_in, bf16[128,8,128]{2,1,0:T(8,128)(2,1)} %get-tuple-element.13.shared_in), custom_call_target="tpu_custom_call" | custom-call | tf_op jit(solution)/shard_map/finish/pallas_call | solution.py:568

commit v5 on v4

--- a/solution.py
+++ b/solution.py
@@ -16,7 +16,7 @@
 
 N_DEV, N_GRP, GRP = 128, 8, 16
 EARLY = 3
-HOLD = 7
+HOLD = 8
 STEPS = ((0, 1), (2, 3), (4, 5, 6, 7))
 OBS, FEAT, HID, CH = 1536, 128, 256, 256
 CAP = 24
@@ -106,7 +106,8 @@
         remote(ref, ref, sem, sem, lat, lon).wait_recv()
 
 
-    dep[...] = jnp.zeros_like(dep)
+    dep[0:1] = jnp.zeros((1, 40, CH), F32)
+    dep[TLAT + 1 :] = jnp.zeros((1, 40, CH), F32)
     recv_cot[0] = jnp.zeros(recv_cot.shape[1:], BF16)
     recv_cot[TLAT + 1] = jnp.zeros(recv_cot.shape[1:], BF16)
 
@@ -116,6 +117,7 @@
         pl.semaphore_signal(barrier, inc=1, device_id=(to_lat, to_lon), device_id_type=MESH)
 
     each_peer(greet)
+    dep[1 : 1 + TLAT, 8 : 8 + TLON, :] = jnp.zeros((TLAT, TLON, CH), F32)
 
 
     for copy in ins[:4]:

time: 47.7 us -> 47.7 us (level)
  no operation moved by 1% of the time
where the time goes in v5:
time: 47.7 us; the launch traced here: 47.5 us
  Pallas kernels  46.1 us (97%)
  between operations  1.45 us (3%)
    pallas_call x1, Pallas kernels, local(): pl.pallas_call(kernel, name='encode_step', out_shape=(jax.ShapeDtypeStruc...  44.2 us
    pallas_call x1, Pallas kernels, local(): pl.pallas_call(finish, name='finish', out_shape=tuple((jax.ShapeDtypeStru...  1.86 us

profile of v5, /device:TPU:1, one launch (start us, length us, event | category | flops | bytes accessed | tf_op | source)
XLA Modules:
  0.0 47.5 jit_solution(988179108053120769)
XLA Ops:
  1.3 44.2 %encode_step.1 = (bf16[16,24,256]{2,1,0:T(8,128)(2,1)}, bf16[128,8,128]{2,1,0:T(8,128)(2,1)}) custom-call(bf16[1536,128]{1,0:T(8,128)(2,1)} %obs_hbm.1, s32[1,1536]{1,0:T(1,128)} %bitcast.7, s32[1536]{0:T(1024)} %cell_hbm.1, s32[1]{0:T(128)S(6)} %copy.15.count_hbm, s32[128,128]{1,0:T(8,128)} %constant.2.clone.order_hbm, bf16[128,256]{1,0:T(8,128)(2,1)} %w_in_hbm.1, ...), custom_call_target="tpu_custom_call" | custom-call | flops 4000000000 | bytes 2000000 | tf_op jit(solution)/shard_map/encode_step/pallas_call | solution.py:514
  45.5 1.9 %finish.1 = (bf16[16,24,256]{2,1,0:T(8,128)(2,1)}, f32[128,256]{1,0:T(8,128)}, f32[1,256]{1,0:T(1,128)}, f32[256,256]{1,0:T(8,128)}, f32[9,256]{1,0:T(8,128)}) custom-call(bf16[16,24,256]{2,1,0:T(8,128)(2,1)} %get-tuple-element.12.grid_in, bf16[128,8,128]{2,1,0:T(8,128)(2,1)} %get-tuple-element.13.shared_in), custom_call_target="tpu_custom_call" | custom-call | tf_op jit(solution)/shard_map/finish/pallas_call | solution.py:570
